TPU v7x, 256 devices: a whole 4x4x8 slice. The times are simulated.
256 devices in a mesh: grp: 4 (over z_lo), slab: 64 (over z_hi, x, y, core).
Axes of the slice: x: 4, y: 4, z: 8 (z_hi: 2, z_lo: 4; z = z_hi * 4 + z_lo), core: 2. Of those that a mesh axis runs over, the one named last changes fastest.
Arguments:
- snapshots: bfloat16 [4, 128, 256, 8, 128], P('grp', None, 'slab'), may hold values from -24 to 24
- base_flow: float32 [256, 8, 128], P('slab'), may hold values from 0.1 to 0.6
Outputs:
- direct_modes: bfloat16 [128, 256, 8, 128], P('grp', 'slab')
- adjoint_modes: bfloat16 [128, 256, 8, 128], P('grp', 'slab')
All inputs are finite; a program needn't handle non-finite values.
Results may differ from a plain program's by a relative error of at most 0.015.
Values may be sent and summed in bfloat16 or wider, within the bound.
A program may use at most 64 MiB of HBM per device.

v0:
```python
import math

import jax
import jax.numpy as jnp
from jax import lax
from jax.sharding import PartitionSpec as P

SNAP = 128
SECTIONS = 4


diffuse_x = 0.35
diffuse_side = 0.05
keep_center = 0.1
damping = 0.5


def with_halo(cells, sides, width):
    for axis, dim in sides:
        count = lax.axis_size(axis)
        head = lax.slice_in_dim(cells, 0, width, axis=dim)
        tail = lax.slice_in_dim(cells, cells.shape[dim] - width, cells.shape[dim], axis=dim)
        cells = jnp.concatenate(
            [
                lax.ppermute(tail, axis, [(i, (i + 1) % count) for i in range(count)]),
                cells,
                lax.ppermute(head, axis, [((i + 1) % count, i) for i in range(count)]),
            ],
            axis=dim,
        )
    return cells


def rows_for(lines, count):
    spare = -len(lines) % count
    return jnp.pad(lines, [(0, spare)] + [(0, 0)] * (lines.ndim - 1))


def from_root(shard, axis, root):
    lines = jnp.where(lax.axis_index(axis) == root, shard, jnp.zeros_like(shard)).reshape(
        -1, *shard.shape[1:][-1:]
    )
    padded = rows_for(lines, lax.axis_size(axis))
    own = lax.psum_scatter(padded, axis, scatter_dimension=0, tiled=True)
    return lax.all_gather(own, axis, axis=0, tiled=True)[: len(lines)].reshape(shard.shape)


def total_of_pieces(shard, axis):
    blocks = lax.all_gather(shard, axis)
    return blocks.sum(axis=0)


def from_everyone(shard, axis):
    copies = jnp.broadcast_to(shard, (lax.axis_size(axis), *shard.shape))
    return lax.all_to_all(copies, axis, split_axis=0, concat_axis=0, tiled=True)


def of_everyone(shard, axis):
    everything = from_everyone(shard, axis)
    return jnp.sum(everything.astype(jnp.float32), axis=0)


def in_blocks(shard, dim, count):
    shape = shard.shape
    blocks = shard.reshape(*shape[:dim], count, shape[dim] // count, *shape[dim + 1 :])
    return jnp.moveaxis(blocks, dim, 0)


def sent_and_summed(shard, axis, dim):
    count = lax.axis_size(axis)
    blocks = lax.all_to_all(in_blocks(shard, dim, count), axis, 0, 0, tiled=True)
    return jnp.sum(blocks.astype(jnp.float32), axis=0)


def advance_section(extended, plus_coef, minus_coef):
    center = extended[:, 1:-1].astype(jnp.float32)
    ahead_cells = extended[:, 2:].astype(jnp.float32)
    behind = extended[:, :-2].astype(jnp.float32)
    side_sum = jnp.roll(center, 1, axis=2) + jnp.roll(center, -1, axis=2)
    side_sum = side_sum + jnp.roll(center, 1, axis=3) + jnp.roll(center, -1, axis=3)
    updated = (
        keep_center * center
        + plus_coef * ahead_cells
        + minus_coef * behind
        + diffuse_side * side_sum
    )
    return updated.astype(jnp.bfloat16)


def blockwise(sweep_block, extended):
    block_size = math.gcd(extended.shape[0], 64)
    blocks = extended.reshape((extended.shape[0] // block_size, block_size) + extended.shape[1:])
    result = lax.map(sweep_block, blocks)
    return result.reshape((extended.shape[0],) + result.shape[2:])


def per_device(snapshots, base_flow):
    snapshot_field = snapshots[0]
    groups = lax.axis_size("grp")
    group_index = lax.axis_index("grp")
    adjoint = group_index == groups - 1
    cell_rows = snapshot_field.shape[1]
    flow_ext = with_halo(base_flow, (("slab", 0),), SECTIONS)
    plus_coef = jnp.where(adjoint, diffuse_x + 0.5 * flow_ext[2:], diffuse_x - 0.5 * flow_ext[1:-1])
    minus_coef = jnp.where(
        adjoint, diffuse_x - 0.5 * flow_ext[:-2], diffuse_x + 0.5 * flow_ext[1:-1]
    )
    extended = with_halo(snapshot_field, (("slab", 1),), SECTIONS)

    def all_sections(snap_block):
        for section_index in range(SECTIONS):
            inner_rows = snap_block.shape[1] - 2
            snap_block = advance_section(
                snap_block,
                plus_coef[section_index : section_index + inner_rows],
                minus_coef[section_index : section_index + inner_rows],
            )
        return snap_block

    snapshot_field = blockwise(all_sections, extended)
    adjoint_field = from_root(snapshot_field, "grp", groups - 1)
    direct_flat = snapshot_field.reshape(SNAP, -1)
    adjoint_flat = adjoint_field.reshape(SNAP, -1)
    partial_value = lax.dot_general(
        adjoint_flat, direct_flat, (((1,), (1,)), ((), ())), preferred_element_type=jnp.float32
    )
    partial_value = jnp.where(adjoint, jnp.float32(0.0), partial_value)
    cell_count = (
        cell_rows * lax.axis_size("slab") * snapshot_field.shape[2] * snapshot_field.shape[3]
    )
    norm_scale = 1.0 / math.sqrt(cell_count)
    coupling = total_of_pieces(partial_value, "slab") * norm_scale
    own_gram = jnp.dot(coupling, coupling.T, precision=lax.Precision.HIGHEST)
    gram_matrix = of_everyone(own_gram.astype(jnp.bfloat16), "grp").astype(jnp.float32)
    energy = jnp.trace(gram_matrix) / SNAP
    system = gram_matrix / energy + damping * jnp.eye(SNAP, dtype=jnp.float32)
    factor = jnp.linalg.cholesky(system)
    inverse = jax.scipy.linalg.cho_solve((factor, True), jnp.eye(SNAP, dtype=jnp.float32))
    weights = (
        jnp.dot(inverse, coupling, precision=lax.Precision.HIGHEST) / jnp.sqrt(energy)
    ).astype(jnp.bfloat16)
    mode_share = SNAP // groups
    row_block = lax.slice_in_dim(weights, 0, mode_share * lax.axis_size("grp"), axis=0)
    summed_modes = sent_and_summed(
        jnp.dot(row_block, direct_flat, preferred_element_type=jnp.float32).astype(jnp.bfloat16),
        "grp",
        0,
    )
    direct_modes = summed_modes.astype(jnp.bfloat16).reshape(
        (mode_share,) + snapshot_field.shape[1:]
    )
    inverse_rows = lax.dynamic_slice_in_dim(
        inverse.astype(jnp.bfloat16), group_index * mode_share, mode_share, 0
    )
    adjoint_modes = jnp.dot(inverse_rows, adjoint_flat, preferred_element_type=jnp.float32)
    adjoint_modes = adjoint_modes.astype(jnp.bfloat16).reshape(
        (mode_share,) + snapshot_field.shape[1:]
    )
    return (direct_modes, adjoint_modes)


def solution(mesh):
    return jax.shard_map(
        per_device,
        mesh=mesh,
        in_specs=(P("grp", None, "slab", None, None), P("slab", None, None)),
        out_specs=(P("grp", "slab", None, None), P("grp", "slab", None, None)),
        check_vma=False,
    )
```

profile of v0, /device:TPU:64, one launch (start us, length us, event | category | flops | bytes accessed | tf_op | source)
XLA Modules:
  0.0 317.3 jit_solution(3666917486311608382)
XLA Ops:
  7.3 9.9 %collective-permute-start.1 = (bf16[128,4,8,128]{3,2,1,0:T(8,128)(2,1)}, bf16[128,4,8,128]{3,2,1,0:T(8,128)(2,1)S(1)}, u32[]{:S(2)}, u32[]{:S(2)}) collective-permute-start(bf16[128,4,8,128]{3,2,1,0:T(8,128)(2,1)} %bitcast.50), channel_id=1, source_target_pairs={{1,0},{2,1},{3,2},{4,3},{5,4},{6,5},{7,6},{8,7},{9,8},{10,9},{11,1... | collective-permute-start | bytes 3145736 | tf_op jit(solution)/shard_map/ppermute | solution.py:27
  17.2 9.9 %collective-permute-start.3 = (f32[4,8,128]{2,1,0:T(8,128)}, f32[4,8,128]{2,1,0:T(8,128)S(1)}, u32[]{:S(2)}, u32[]{:S(2)}) collective-permute-start(f32[4,8,128]{2,1,0:T(8,128)} %param.5), channel_id=1, source_target_pairs={{1,0},{2,1},{3,2},{4,3},{5,4},{6,5},{7,6},{8,7},{9,8},{10,9},{11,1... | collective-permute-start | bytes 49160 | tf_op jit(solution)/shard_map/ppermute | solution.py:27
  27.0 14.5 %collective-permute-done.2 = f32[4,8,128]{2,1,0:T(8,128)S(1)} collective-permute-done((f32[4,8,128]{2,1,0:T(8,128)}, f32[4,8,128]{2,1,0:T(8,128)S(1)}, u32[]{:S(2)}, u32[]{:S(2)}) %collective-permute-start.2) | collective-permute-done | bytes 16416 | tf_op jit(solution)/shard_map/ppermute | solution.py:25
  41.6 0.7 constant_dynamic-update-slice_fusion.1
  42.4 0.9 copy-done
  43.7 2.0 pad_maximum_fusion
  45.7 35.1 %while.11 = (s32[]{:T(128)}, bf16[2,64,4,8,128]{4,3,2,1,0:T(8,128)(2,1)}, bf16[2,64,12,8,128]{4,3,2,1,0:T(8,128)(2,1)S(1)}, f32[10,8,128]{2,1,0:T(8,128)S(1)}, f32[10,8,128]{2,1,0:T(8,128)S(1)}) while((s32[]{:T(128)}, bf16[2,64,4,8,128]{4,3,2,1,0:T(8,128)(2,1)}, bf16[2,64,12,8,128]{4,3,2,1,0:T(8,128)(2,1)S(1)}, ...), condition=%wide.region_1.2_spmd.clone, body=%wide.region_0.1_spmd.sunk.clone | while | flops 34865152 | bytes 117441088 | solution.py:93
  46.5 0.8 fusion.103
  47.4 0.8 fusion.104
  48.6 2.9 fusion.105
  51.7 0.5 fusion.106
  52.3 0.7 fusion.108
  53.0 0.7 fusion.109
  54.1 2.4 fusion.110
  56.9 0.5 fusion.113
  57.4 0.5 fusion.114
  58.2 1.9 fusion.115
  61.4 1.9 bitcast_dynamic-update-slice_fusion.3
  63.9 0.8 fusion.103
  64.8 0.8 fusion.104
  66.0 2.9 fusion.105
  69.2 0.5 fusion.106
  69.7 0.7 fusion.108
  70.4 0.7 fusion.109
  71.5 2.4 fusion.110
  74.3 0.5 fusion.113
  74.8 0.5 fusion.114
  75.6 1.9 fusion.115
  78.8 1.9 bitcast_dynamic-update-slice_fusion.3
  80.7 1.1 broadcast_select_fusion
  81.9 32.8 %reduce-scatter.2.cloned.1.call-done = bf16[1024,128]{1,0:T(8,128)(2,1)} async-done(((bf16[4096,128]{1,0:T(8,128)(2,1)}), bf16[1024,128]{1,0:T(8,128)(2,1)}) %reduce-scatter.2.cloned.1.call-update) | async-done | bytes 262160 | tf_op jit(solution)/shard_map/reduce_scatter | solution.py:44
  114.7 1.5 reshape_reshape.7
  116.3 32.7 %all-gather.4.cloned.1.call-done = bf16[4096,128]{1,0:T(8,128)(2,1)} async-done(((bf16[1024,128]{1,0:T(8,128)(2,1)}), bf16[4096,128]{1,0:T(8,128)(2,1)}) %all-gather.4.cloned.1.call-update) | async-done | bytes 1048592 | tf_op jit(solution)/shard_map/all_gather | solution.py:45
  148.9 1.5 reshape_reshape.6
  150.5 1.1 convolution_select_fusion
  151.6 92.7 %all-gather.6.cloned.1.call-done = f32[8192,128]{1,0:T(8,128)} async-done(((f32[128,128]{1,0:T(8,128)}), f32[8192,128]{1,0:T(8,128)}) %all-gather.6.cloned.1.call-update) | async-done | bytes 4194320 | tf_op jit(solution)/shard_map/all_gather | solution.py:49
  244.2 2.4 reduce_sum.40
  246.9 9.1 %all_to_all.10 = bf16[4,128,128]{2,1,0:T(8,128)(2,1)S(1)} all-to-all(bf16[4,128,128]{2,1,0:T(8,128)(2,1)S(1)} %broadcast_in_dim.25), channel_id=1, replica_groups=mesh['grp'=4,'slab'=64] {'grp'}, dimensions={0} | all-to-all | bytes 262144 | tf_op jit(solution)/shard_map/all_to_all | solution.py:55
  256.0 0.6 select_reduce_fusion.1
  257.6 11.7 %cholesky.18 = f32[128,128]{1,0:T(8,128)S(1)} custom-call(f32[128,128]{1,0:T(8,128)S(1)} %fusion.28), custom_call_target="Cholesky" | custom-call | tf_op jit(solution)/shard_map/jit(cholesky)/cholesky | solution.py:137
  269.3 0.6 compare_reduce_fusion
  270.0 0.7 fusion.22
  270.6 9.8 %custom-call.10 = f32[1,128,128]{1,2,0:T(8,128)S(1)} custom-call(f32[1,128,128]{2,1,0:T(8,128)S(1)} %fusion.22), custom_call_target="InvertDiagBlocksLowerTriangular" | custom-call | tf_op jit(solution)/shard_map/jit(_cho_solve)/triangular_solve | solution.py:138
  281.1 1.4 convolution_convert_fusion
  282.5 5.7 %all-to-all-start.1 = ((bf16[4,32,4096]{2,1,0:T(8,128)(2,1)}), bf16[4,32,4096]{2,1,0:T(8,128)(2,1)S(1)}, u32[]{:S(2)}, u32[]{:S(2)}) async-start(bf16[4,32,4096]{2,1,0:T(8,128)(2,1)} %bitcast.11), calls=%async_computation.2 | async-start | bytes 2097152 | tf_op jit(solution)/shard_map/all_to_all | solution.py:71
  288.5 0.7 copy.10
  289.2 20.6 %all-to-all-done.1 = bf16[4,32,4096]{2,1,0:T(8,128)(2,1)S(1)} async-done(((bf16[4,32,4096]{2,1,0:T(8,128)(2,1)}), bf16[4,32,4096]{2,1,0:T(8,128)(2,1)S(1)}, u32[]{:S(2)}, u32[]{:S(2)}) %all-to-all-start.1) | async-done | bytes 1048608 | tf_op jit(solution)/shard_map/all_to_all | solution.py:71
  310.1 0.7 copy.9
  (71 shorter events, 9.3 us)
Async XLA Ops:
  7.2 107.5 %reduce-scatter.2.cloned.1.call-start = ((), (), s32[]{:S(2)}) async-start(), calls=%async_computation.3 | async-start | bytes 1310720 | tf_op jit(solution)/shard_map/reduce_scatter | solution.py:44
  7.2 35.1 %collective-permute-start = (bf16[128,4,8,128]{3,2,1,0:T(8,128)(2,1)}, bf16[128,4,8,128]{3,2,1,0:T(8,128)(2,1)S(1)}, u32[]{:S(2)}, u32[]{:S(2)}) collective-permute-start(bf16[128,4,8,128]{3,2,1,0:T(8,128)(2,1)} %bitcast.49), channel_id=1, source_target_pairs={{0,1},{1,2},{2,3},{3,4},{4,5},{5,6},{6,7},{7,8},{8,9},{9,10},{10,1... | collective-permute-start | bytes 3145736 | tf_op jit(solution)/shard_map/ppermute | solution.py:25
  7.3 35.0 %collective-permute-start.1 = (bf16[128,4,8,128]{3,2,1,0:T(8,128)(2,1)}, bf16[128,4,8,128]{3,2,1,0:T(8,128)(2,1)S(1)}, u32[]{:S(2)}, u32[]{:S(2)}) collective-permute-start(bf16[128,4,8,128]{3,2,1,0:T(8,128)(2,1)} %bitcast.50), channel_id=1, source_target_pairs={{1,0},{2,1},{3,2},{4,3},{5,4},{6,5},{7,6},{8,7},{9,8},{10,9},{11,1... | collective-permute-start | bytes 3145736 | tf_op jit(solution)/shard_map/ppermute | solution.py:27
  17.2 24.4 %collective-permute-start.2 = (f32[4,8,128]{2,1,0:T(8,128)}, f32[4,8,128]{2,1,0:T(8,128)S(1)}, u32[]{:S(2)}, u32[]{:S(2)}) collective-permute-start(f32[4,8,128]{2,1,0:T(8,128)} %param.5), channel_id=1, source_target_pairs={{0,1},{1,2},{2,3},{3,4},{4,5},{5,6},{6,7},{7,8},{8,9},{9,10},{10,1... | collective-permute-start | bytes 49160 | tf_op jit(solution)/shard_map/ppermute | solution.py:25
  17.2 25.1 %collective-permute-start.3 = (f32[4,8,128]{2,1,0:T(8,128)}, f32[4,8,128]{2,1,0:T(8,128)S(1)}, u32[]{:S(2)}, u32[]{:S(2)}) collective-permute-start(f32[4,8,128]{2,1,0:T(8,128)} %param.5), channel_id=1, source_target_pairs={{1,0},{2,1},{3,2},{4,3},{5,4},{6,5},{7,6},{8,7},{9,8},{10,9},{11,1... | collective-permute-start | bytes 49160 | tf_op jit(solution)/shard_map/ppermute | solution.py:27
  42.3 1.0 copy-start
  42.4 1.3 copy-start.1
  81.8 67.1 %all-gather.4.cloned.1.call-start = ((), (), s32[]{:S(2)}) async-start(), calls=%async_computation.4 | async-start | bytes 1310720 | tf_op jit(solution)/shard_map/all_gather | solution.py:45
  114.7 129.5 %all-gather.6.cloned.1.call-start = ((), (), s32[]{:S(2)}) async-start(), calls=%async_computation.5 | async-start | bytes 4259840 | tf_op jit(solution)/shard_map/all_gather | solution.py:49
  282.5 27.3 %all-to-all-start.1 = ((bf16[4,32,4096]{2,1,0:T(8,128)(2,1)}), bf16[4,32,4096]{2,1,0:T(8,128)(2,1)S(1)}, u32[]{:S(2)}, u32[]{:S(2)}) async-start(bf16[4,32,4096]{2,1,0:T(8,128)(2,1)} %bitcast.11), calls=%async_computation.2 | async-start | bytes 2097152 | tf_op jit(solution)/shard_map/all_to_all | solution.py:71
Sparse Core Ops, SparseCore 0:
  81.9 32.6 reduce-scatter.1
  116.5 32.4 all-gather.3
  153.2 91.0 all-gather.5
where the time goes:
time: 321 us; the launch traced here: 317 us
  waiting for transfers between devices  193 us (60%)
  other arithmetic  48.8 us (15%)
  starting transfers between devices  25.6 us (8%)
  local copies, waits for them, and re-layouts  21.6 us (7%)
  between operations  14.6 us (5%)
  blocking collectives  9.05 us (3%)
  matrix products  3.67 us (1%)
    all_gather x1, waiting for transfers between devices, total_of_pieces(): blocks = lax.all_gather(shard, axis)  92.7 us
    reduce_scatter x1, waiting for transfers between devices, from_root(): own = lax.psum_scatter(padded, axis, scatter_dimension=0, tiled=True)  32.8 us
    all_gather x1, waiting for transfers between devices, from_root(): lax.all_gather(own, axis, axis=0, tiled=True)[:len(lines)]  32.7 us
    all_to_all x1, waiting for transfers between devices, sent_and_summed(): lax.all_to_all(in_blocks(shard, dim, count), axis, 0, 0, tiled=True)  20.6 us
    ppermute x2, starting transfers between devices, with_halo(): lax.ppermute(head, axis, [((i + 1) % count, i) for i in range(count)])  19.7 us
    ppermute x2, waiting for transfers between devices, with_halo(): lax.ppermute(tail, axis, [(i, (i + 1) % count) for i in range(count)])  14.5 us
    convert_element_type x6, other arithmetic, advance_section(): return updated.astype(jnp.bfloat16)  14.3 us
    another operation x3, other arithmetic, per_device(): factor = jnp.linalg.cholesky(system)  12.4 us
  transfers between devices with their start and end apart: 8, of which 5 were waited for; matrix products, arithmetic and copies ran while one was open for 1% of the time, Pallas kernels for 0%

commit v1 on v0

v1 whole, which is shorter than its diff:
```python
import functools
import math

import jax
import jax.numpy as jnp
from jax import lax
from jax.experimental import pallas as pl
from jax.experimental.pallas import tpu as pltpu
from jax.sharding import PartitionSpec as P

SNAP = 128
SECTIONS = 4
CHUNKS = 8
PER = SNAP // CHUNKS
MESH = pl.DeviceIdType.MESH
MIB = 1 << 20

diffuse_x = 0.35
diffuse_side = 0.05
keep_center = 0.1
damping = 0.5


def remote(src, dst, send_sem, recv_sem, device):
    return pltpu.make_async_remote_copy(
        src_ref=src, dst_ref=dst, send_sem=send_sem, recv_sem=recv_sem, device_id=device, device_id_type=MESH
    )


def place():
    g = lax.axis_index("grp")
    s = lax.axis_index("slab")
    core = lax.rem(s, 2)
    plane = lax.rem(lax.div(s, 2), 16)
    zh = lax.div(s, 32)
    return g, s, core, plane, zh


def slab_of(zh, plane, core):
    return zh * 32 + plane * 2 + core


def gather_kernel(
    scale,
    u_ref,
    v_ref,
    direct_ref,
    adj_ref,
    coup_ref,
    left,
    right,
    vleft,
    vright,
    cp,
    cm,
    stage,
    part,
    rs_buf,
    tile,
    zbuf,
    mine,
    h_send,
    h_recv,
    v_send,
    v_recv,
    a_send,
    a_recv,
    p_send,
    p_recv,
    z_send,
    z_recv,
    g_send,
    g_recv,
):
    g, s, core, plane, zh = place()
    ahead = lax.rem(s + 1, 64)
    back = lax.rem(s + 63, 64)
    adjoint = g == 3

    barrier = pltpu.get_barrier_semaphore()
    for other in (ahead, back):
        pl.semaphore_signal(barrier, inc=1, device_id=(g, other), device_id_type=MESH)
    for d in range(1, 16):
        pl.semaphore_signal(
            barrier, inc=1, device_id=(g, slab_of(zh, lax.rem(plane + d, 16), core)), device_id_type=MESH
        )
    for d in range(1, 16):
        g2 = lax.rem(g + d // 4, 4)
        zh2 = lax.rem(zh + (d // 2) % 2, 2)
        c2 = lax.rem(core + d % 2, 2)
        pl.semaphore_signal(barrier, inc=1, device_id=(g2, slab_of(zh2, plane, c2)), device_id_type=MESH)
    pl.semaphore_wait(barrier, 32)

    flow = [
        remote(v_ref, vleft, v_send.at[0], v_recv.at[0], (g, ahead)),
        remote(v_ref, vright, v_send.at[1], v_recv.at[1], (g, back)),
    ]
    for copy in flow:
        copy.start()

    def halo(c):
        rows = pl.ds(c * PER, PER)
        return [
            remote(u_ref.at[rows], left.at[rows], h_send.at[0, c], h_recv.at[0, c], (g, ahead)),
            remote(u_ref.at[rows], right.at[rows], h_send.at[1, c], h_recv.at[1, c], (g, back)),
        ]

    def start_halo(c, carry):
        for copy in halo(c):
            copy.start()
        return carry

    lax.fori_loop(0, CHUNKS, start_halo, 0)
    for copy in flow:
        copy.wait()

    v = [vleft[k] for k in range(4)] + [v_ref[k] for k in range(4)] + [vright[k] for k in range(4)]
    for k in range(10):
        cp[k] = jnp.where(adjoint, diffuse_x + 0.5 * v[k + 2], diffuse_x - 0.5 * v[k + 1])
        cm[k] = jnp.where(adjoint, diffuse_x - 0.5 * v[k], diffuse_x + 0.5 * v[k + 1])

    def sections(snap, base):
        rows = [ref[snap, k].astype(jnp.float32) for ref in (left, u_ref, right) for k in range(4)]
        for section in range(SECTIONS):
            new = []
            for k in range(len(rows) - 2):
                center = rows[k + 1]
                side = pltpu.roll(center, 1, 0) + pltpu.roll(center, 7, 0)
                side = side + pltpu.roll(center, 1, 1) + pltpu.roll(center, 127, 1)
                new.append(
                    keep_center * center
                    + cp[section + k] * rows[k + 2]
                    + cm[section + k] * rows[k]
                    + diffuse_side * side
                )
            rows = new
        for k in range(4):
            stage[pl.ds(base + k * 64, 8, stride=8), :] = rows[k]

    def chain(c):
        return remote(
            adj_ref.at[c], adj_ref.at[c], a_send.at[c], a_recv.at[c], (lax.max(g - 1, 0), s)
        )

    def relay(c):
        @pl.when((g == 1) | (g == 2))
        def _():
            chain(c).wait_recv()
            chain(c).start()

    def chunk(c, carry):
        for copy in halo(c):
            copy.wait_recv()

        def one(i, inner):
            for half in range(2):
                sections(c * PER + half * 8 + i, half * 256 + i)
            return inner

        lax.fori_loop(0, 8, one, 0)

        def packed(q):
            low = stage[q * 8 : q * 8 + 8, :]
            high = stage[256 + q * 8 : 256 + q * 8 + 8, :]
            return jnp.concatenate([low, high], axis=0).astype(jnp.bfloat16)

        @pl.when(adjoint)
        def _():
            for q in range(32):
                adj_ref[c, q] = packed(q)
            chain(c).start()

        @pl.when(jnp.logical_not(adjoint))
        def _():
            for q in range(32):
                direct_ref[c, q] = packed(q)

        @pl.when(c >= 1)
        def _():
            relay(c - 1)

        return carry

    lax.fori_loop(0, CHUNKS, chunk, 0)
    relay(CHUNKS - 1)

    @pl.when(g == 0)
    def _():
        for c in range(CHUNKS):
            chain(c).wait_recv()

    def plane_peer(d):
        return lax.rem(plane + d, 16)

    def scatter(d):
        p2 = plane_peer(d)
        return remote(
            part.at[p2], rs_buf.at[plane], p_send.at[p2], p_recv.at[plane], (g, slab_of(zh, p2, core))
        )

    def scatter_in(d):
        p2 = plane_peer(d)
        return remote(
            part.at[plane], rs_buf.at[p2], p_send.at[plane], p_recv.at[p2], (g, slab_of(zh, p2, core))
        )

    slot = g * 4 + zh * 2 + core

    def peer16(d):
        g2 = lax.rem(g + d // 4, 4)
        zh2 = lax.rem(zh + (d // 2) % 2, 2)
        c2 = lax.rem(core + d % 2, 2)
        return g2, zh2, c2

    def spread(d):
        g2, zh2, c2 = peer16(d)
        return remote(
            tile, zbuf.at[slot], z_send.at[d], z_recv.at[slot], (g2, slab_of(zh2, plane, c2))
        )

    @pl.when(jnp.logical_not(adjoint))
    def _():
        def product(q, acc):
            lhs = [adj_ref[:, 2 * q + j].reshape(SNAP, 128) for j in range(2)]
            rhs = [direct_ref[:, 2 * q + j].reshape(SNAP, 128) for j in range(2)]
            return acc + lax.dot_general(
                jnp.concatenate(lhs, axis=1),
                jnp.concatenate(rhs, axis=1),
                (((1,), (1,)), ((), ())),
                preferred_element_type=jnp.float32,
            )

        total = lax.fori_loop(0, 16, product, jnp.zeros((SNAP, SNAP), jnp.float32))
        part[...] = total.reshape(16, 8, SNAP)
        for d in range(1, 16):
            scatter(d).start()
        rs_buf[plane] = part[plane]
        for d in range(1, 16):
            scatter_in(d).wait_recv()
        tile[...] = jnp.sum(rs_buf[...], axis=0)
        for d in range(1, 16):
            spread(d).start()
        zbuf[slot] = tile[...]

    for g2 in range(3):
        for k in range(4):
            here = g2 * 4 + k

            @pl.when(slot != here)
            def _():
                pltpu.make_async_copy(zbuf.at[here], zbuf.at[here], z_recv.at[here]).wait()

    for g2 in range(3):
        mine[g2] = jnp.sum(zbuf[g2 * 4 : g2 * 4 + 4], axis=0) * scale

    def share(d):
        p2 = plane_peer(d)
        return remote(
            mine, coup_ref.at[plane], g_send.at[p2], g_recv.at[plane], (g, slab_of(zh, p2, core))
        )

    def share_in(d):
        p2 = plane_peer(d)
        return remote(mine, coup_ref.at[p2], g_send.at[plane], g_recv.at[p2], (g, slab_of(zh, p2, core)))

    for d in range(1, 16):
        share(d).start()
    coup_ref[plane] = mine[...]
    for d in range(1, 16):
        share_in(d).wait_recv()

    def drain(c, carry):
        for copy in halo(c):
            copy.wait_send()

        @pl.when(g > 0)
        def _():
            chain(c).wait_send()

        return carry

    lax.fori_loop(0, CHUNKS, drain, 0)
    for d in range(1, 16):
        share(d).wait_send()

    @pl.when(jnp.logical_not(adjoint))
    def _():
        for d in range(1, 16):
            scatter(d).wait_send()
            spread(d).wait_send()


def inverse_kernel(coup_ref, weights_ref, inverse_ref, m_ref):
    g = lax.axis_index("grp")
    gram = jnp.zeros((SNAP, SNAP), jnp.float32)
    for k in range(3):
        c = coup_ref[:, k].reshape(SNAP, SNAP)
        gram = gram + lax.dot_general(
            c, c, (((1,), (1,)), ((), ())), precision=lax.Precision.HIGHEST, preferred_element_type=jnp.float32
        )
    row = lax.broadcasted_iota(jnp.int32, (SNAP, SNAP), 0)
    col = lax.broadcasted_iota(jnp.int32, (SNAP, SNAP), 1)
    eye = (row == col).astype(jnp.float32)
    energy = jnp.sum(gram * eye, axis=(0, 1), keepdims=True) / SNAP
    m_ref[...] = gram / energy + damping * eye

    sub = lax.broadcasted_iota(jnp.int32, (8, SNAP), 0)
    lane = lax.broadcasted_iota(jnp.int32, (8, SNAP), 1)

    def spread_row(x, j):
        return jnp.broadcast_to(x[j : j + 1, :], (8, SNAP))

    for b in range(16):
        full = m_ref[...]
        columns = [jnp.broadcast_to(full[:, 8 * b + j : 8 * b + j + 1], (SNAP, SNAP)) for j in range(8)]
        panel = full[8 * b : 8 * b + 8, :]
        pivots = [c[8 * b : 8 * b + 8, :] for c in columns]
        for j in range(8):
            own = sub == j
            inv = 1.0 / spread_row(pivots[j], j)
            pj = pivots[j]
            panel = jnp.where(lane == 8 * b + j, own.astype(jnp.float32), panel)
            new = spread_row(panel, j) * inv
            panel = jnp.where(own, new, panel - pj * new)
            for i in range(j + 1, 8):
                new = spread_row(pivots[i], j) * inv
                pivots[i] = jnp.where(own, new, pivots[i] - pj * new)
        inside = (lane >= 8 * b) & (lane < 8 * b + 8)
        spread = [spread_row(panel, j) for j in range(8)]
        for t in range(16):
            if t == b:
                m_ref[8 * t : 8 * t + 8, :] = panel
            else:
                rest = jnp.where(inside, 0.0, full[8 * t : 8 * t + 8, :])
                for j in range(8):
                    rest = rest - columns[j][8 * t : 8 * t + 8, :] * spread[j]
                m_ref[8 * t : 8 * t + 8, :] = rest
    inverse = m_ref[...]
    inverse_ref[...] = inverse.astype(jnp.bfloat16)
    own = coup_ref[:, lax.min(g, 2)].reshape(SNAP, SNAP)
    weights = jnp.dot(
        inverse, own, precision=lax.Precision.HIGHEST, preferred_element_type=jnp.float32
    ) / jnp.sqrt(energy)
    weights_ref[...] = weights.astype(jnp.bfloat16)


def modes_kernel(
    direct_ref, adj_ref, weights_ref, inverse_ref, dm_ref, am_ref, terms, inbox, t_send, t_recv
):
    g, s, core, plane, zh = place()
    adjoint = g == 3
    barrier = pltpu.get_barrier_semaphore()
    for d in range(1, 4):
        pl.semaphore_signal(barrier, inc=1, device_id=(lax.rem(g + d, 4), s), device_id_type=MESH)

    def rows_of(ref, q):
        return ref[:, q].reshape(SNAP, 128)

    @pl.when(jnp.logical_not(adjoint))
    def _():
        def product(q, carry):
            rhs = jnp.concatenate([rows_of(direct_ref, 2 * q + j) for j in range(2)], axis=1)
            out = jnp.dot(weights_ref[...], rhs, preferred_element_type=jnp.float32).astype(jnp.bfloat16)
            for j in range(2):
                terms[:, 2 * q + j] = out[:, j * 128 : j * 128 + 128].reshape(4, 32, 128)
            return carry

        lax.fori_loop(0, 16, product, 0)

    pl.semaphore_wait(barrier, 3)

    def send(r):
        return remote(terms.at[r], inbox.at[g], t_send.at[r], t_recv.at[g], (r, s))

    for r in (3, 0, 2, 1):

        @pl.when(jnp.logical_not(adjoint) & (g != r))
        def _():
            send(r).start()

    own = inverse_ref[pl.ds(pl.multiple_of(g * 32, 32), 32), :]

    def adjoint_product(q, carry):
        rhs = jnp.concatenate([rows_of(adj_ref, 2 * q + j) for j in range(2)], axis=1)
        out = jnp.dot(own, rhs, preferred_element_type=jnp.float32).astype(jnp.bfloat16)
        for j in range(2):
            am_ref[2 * q + j] = out[:, j * 128 : j * 128 + 128]
        return carry

    lax.fori_loop(0, 16, adjoint_product, 0)

    for k in range(3):

        @pl.when(g != k)
        def _():
            pltpu.make_async_copy(inbox.at[k], inbox.at[k], t_recv.at[k]).wait()

        @pl.when(g == k)
        def _():
            inbox[k] = terms[k]

    def total(q, carry):
        acc = inbox[0, q].astype(jnp.float32)
        for k in (1, 2):
            acc = acc + inbox[k, q].astype(jnp.float32)
        dm_ref[q] = acc.astype(jnp.bfloat16)
        return carry

    lax.fori_loop(0, 32, total, 0, unroll=4)
    for r in range(4):

        @pl.when(jnp.logical_not(adjoint) & (g != r))
        def _():
            send(r).wait_send()


def per_device(snapshots, base_flow):
    field = snapshots[0]
    f32, bf16 = jnp.float32, jnp.bfloat16
    vmem = pl.BlockSpec(memory_space=pltpu.VMEM)
    dma = pltpu.SemaphoreType.DMA
    slab_shape = field.shape
    cells = 64 * math.prod(slab_shape[1:])
    scale = 1.0 / math.sqrt(cells)
    packed = jax.ShapeDtypeStruct((CHUNKS, 32, PER, 128), bf16)
    direct, adj, coup = pl.pallas_call(
        functools.partial(gather_kernel, scale),
        out_shape=(packed, packed, jax.ShapeDtypeStruct((16, 3, 8, SNAP), f32)),
        in_specs=[vmem] * 2,
        out_specs=(vmem,) * 3,
        scratch_shapes=[
            pltpu.VMEM(slab_shape, bf16),
            pltpu.VMEM(slab_shape, bf16),
            pltpu.VMEM((4, 8, 128), f32),
            pltpu.VMEM((4, 8, 128), f32),
            pltpu.VMEM((10, 8, 128), f32),
            pltpu.VMEM((10, 8, 128), f32),
            pltpu.VMEM((512, 128), f32),
            pltpu.VMEM((16, 8, SNAP), f32),
            pltpu.VMEM((16, 8, SNAP), f32),
            pltpu.VMEM((8, SNAP), f32),
            pltpu.VMEM((12, 8, SNAP), f32),
            pltpu.VMEM((3, 8, SNAP), f32),
            dma((2, CHUNKS)),
            dma((2, CHUNKS)),
            dma((2,)),
            dma((2,)),
            dma((CHUNKS,)),
            dma((CHUNKS,)),
            dma((16,)),
            dma((16,)),
            dma((16,)),
            dma((12,)),
            dma((16,)),
            dma((16,)),
        ],
        compiler_params=pltpu.CompilerParams(
            collective_id=0, has_side_effects=True, vmem_limit_bytes=40 * MIB
        ),
        name="gather",
    )(field, base_flow)
    weights, inverse = pl.pallas_call(
        inverse_kernel,
        out_shape=(jax.ShapeDtypeStruct((SNAP, SNAP), bf16),) * 2,
        in_specs=[vmem],
        out_specs=(vmem,) * 2,
        scratch_shapes=[pltpu.VMEM((SNAP, SNAP), f32)],
        name="inverse",
    )(coup)
    modes = jax.ShapeDtypeStruct((32, 32, 128), bf16)
    dm, am = pl.pallas_call(
        modes_kernel,
        out_shape=(modes, modes),
        in_specs=[vmem] * 4,
        out_specs=(vmem,) * 2,
        scratch_shapes=[
            pltpu.VMEM((4, 32, 32, 128), bf16),
            pltpu.VMEM((3, 32, 32, 128), bf16),
            dma((4,)),
            dma((3,)),
        ],
        compiler_params=pltpu.CompilerParams(
            collective_id=1, has_side_effects=True, vmem_limit_bytes=40 * MIB
        ),
        name="modes",
    )(direct, adj, weights, inverse)

    def placed(x):
        return x.reshape(4, 8, 32, 128).transpose(2, 0, 1, 3)

    return placed(dm), placed(am)


def solution(mesh):
    return jax.shard_map(
        per_device,
        mesh=mesh,
        in_specs=(P("grp", None, "slab", None, None), P("slab", None, None)),
        out_specs=(P("grp", "slab", None, None), P("grp", "slab", None, None)),
        check_vma=False,
    )
```

time: 321 us -> 128 us (0.40); the launches traced: 317 us -> 128 us
  waiting for transfers between devices: 193 us -> 0 us
  Pallas kernels: 0 us -> 122 us
  other arithmetic: 48.8 us -> 0 us
  starting transfers between devices: 25.6 us -> 0 us
  local copies, waits for them, and re-layouts: 21.6 us -> 5.11 us
  between operations: 14.6 us -> 0.67 us
  blocking collectives: 9.05 us -> 0 us
  matrix products: 3.67 us -> 0 us
    all_gather x2 -> x0, waiting for transfers between devices: 125 us -> none  [the longest x1 92.7 us: total_of_pieces(): blocks = lax.all_gather(shard, axis)]
    pallas_call x0 -> x3, Pallas kernels: none -> 122 us  [the longest x1 90.4 us: per_device(): pl.pallas_call(functools.partial(gather_kernel, scale), out_shape=(packed...]
    reduce_scatter x1 -> x0, waiting for transfers between devices: 32.8 us -> none  [from_root(): own = lax.psum_scatter(padded, axis, scatter_dimension=0, tiled=True)]
    another operation x5 -> x0, other arithmetic: 22.9 us -> none  [the longest x3 12.4 us: per_device(): factor = jnp.linalg.cholesky(system)]
    all_to_all x1 -> x0, waiting for transfers between devices: 20.6 us -> none  [sent_and_summed(): lax.all_to_all(in_blocks(shard, dim, count), axis, 0, 0, tiled=True)]
    ppermute x4 -> x0, starting transfers between devices: 19.8 us -> none  [the longest x2 19.7 us: with_halo(): lax.ppermute(head, axis, [((i + 1) % count, i) for i in range(count)])]
    convert_element_type x14 -> x0, other arithmetic: 15.7 us -> none  [the longest x6 14.3 us: advance_section(): return updated.astype(jnp.bfloat16)]
    slice x44 -> x0, local copies, waits for them, and re-layouts: 14.7 us -> none  [the longest x12 8.29 us: advance_section(): jnp.roll(center, -1, axis=3)]
  transfers between devices with their start and end apart: 8 -> 0, of which waited for: 5 -> 0; matrix products, arithmetic and copies ran while one was open for 1% -> 0% of each run, Pallas kernels for 0% -> 0%
where the time goes in v1:
time: 128 us
  Pallas kernels  122 us (95%)
  local copies, waits for them, and re-layouts  5.11 us (4%)
    pallas_call x1, Pallas kernels, per_device(): pl.pallas_call(functools.partial(gather_kernel, scale), out_shape=(packed...  90.4 us
    pallas_call x1, Pallas kernels, per_device(): pl.pallas_call(modes_kernel, out_shape=(modes, modes), in_specs=[vmem] *...  25.4 us
    pallas_call x1, Pallas kernels, per_device(): pl.pallas_call(inverse_kernel, out_shape=(jax.ShapeDtypeStruct((SNAP, SNA...  6.5 us
    unnamed x10, local copies, waits for them, and re-layouts  4.12 us

profile of v1, /device:TPU:64, one launch (start us, length us, event | category | flops | bytes accessed | tf_op | source)
XLA Modules:
  0.0 128.0 jit_solution(4697243122098597745)
XLA Ops:
  0.6 0.0 copy-start
  0.6 1.2 copy-done
  1.9 0.0 copy-start.4
  1.9 0.7 copy-done.4
  2.6 90.4 %gather.1 = (bf16[8,32,16,128]{3,2,1,0:T(8,128)(2,1)S(1)}, bf16[8,32,16,128]{3,2,1,0:T(8,128)(2,1)S(1)}, f32[16,3,8,128]{3,2,1,0:T(8,128)S(1)}) custom-call(bf16[128,4,8,128]{3,2,1,0:T(8,128)(2,1)S(1)} %bitcast.7, f32[4,8,128]{2,1,0:T(8,128)S(1)} %copy-done.4), custom_call_target="tpu_custom_call" | custom-call | tf_op jit(solution)/shard_map/gather/pallas_call | solution.py:426
  92.9 0.0 copy-start.1
  92.9 0.7 copy-done.1
  93.6 6.5 %inverse.1 = (bf16[128,128]{1,0:T(8,128)(2,1)}, bf16[128,128]{1,0:T(8,128)(2,1)}) custom-call(f32[16,3,8,128]{3,2,1,0:T(8,128)} %copy-done.1), custom_call_target="tpu_custom_call" | custom-call | tf_op jit(solution)/shard_map/inverse/pallas_call | solution.py:462
  100.1 0.0 copy-start.2
  100.1 0.8 copy-done.2
  100.9 0.0 copy-start.3
  100.9 0.8 copy-done.3
  101.6 25.4 %modes.1 = (bf16[32,32,128]{2,1,0:T(8,128)(2,1)S(1)}, bf16[32,32,128]{2,1,0:T(8,128)(2,1)S(1)}) custom-call(bf16[8,32,16,128]{3,2,1,0:T(8,128)(2,1)S(1)} %get-tuple-element.9.direct_ref, bf16[8,32,16,128]{3,2,1,0:T(8,128)(2,1)S(1)} %get-tuple-element.10.adj_ref, bf16[128,128]{1,0:T(8,128)(2,1)S(1)} %copy-done.2, bf16[128,128]{1,0:T(8,128)(2,1)S(1)} %copy-done.3), custom_call_target="tpu_custom_call" | custom-call | tf_op jit(solution)/shard_map/modes/pallas_call | solution.py:471
  127.0 1.0 copy_bitcast_fusion
Async XLA Ops:
  0.6 1.2 copy-start
  1.9 0.7 copy-start.4
  92.9 0.7 copy-start.1
  100.1 0.8 copy-start.2
  100.9 0.8 copy-start.3

commit v2 on v1

v2 whole, which is shorter than its diff:
```python
import functools
import math

import jax
import jax.numpy as jnp
from jax import lax
from jax.experimental import pallas as pl
from jax.experimental.pallas import tpu as pltpu
from jax.sharding import PartitionSpec as P

SNAP = 128
SECTIONS = 4
CHUNKS = 8
PER = SNAP // CHUNKS
MESH = pl.DeviceIdType.MESH
MIB = 1 << 20
EARLY = 2

diffuse_x = 0.35
diffuse_side = 0.05
keep_center = 0.1
damping = 0.5


def remote(src, dst, send_sem, recv_sem, device):
    return pltpu.make_async_remote_copy(
        src_ref=src, dst_ref=dst, send_sem=send_sem, recv_sem=recv_sem, device_id=device, device_id_type=MESH
    )


def place():
    g = lax.axis_index("grp")
    s = lax.axis_index("slab")
    core = lax.rem(s, 2)
    plane = lax.rem(lax.div(s, 2), 16)
    zh = lax.div(s, 32)
    return g, s, core, plane, zh


def slab_of(zh, plane, core):
    return zh * 32 + plane * 2 + core


def kernel(
    scale,
    u_ref,
    v_ref,
    dm_ref,
    am_ref,
    left,
    right,
    relay_buf,
    vleft,
    vright,
    cp,
    cm,
    stage,
    fields,
    adj_ref,
    part,
    rs_buf,
    tile,
    zbuf,
    mine,
    coup_ref,
    m_ref,
    acc,
    terms,
    inbox,
    h_send,
    h_recv,
    v_send,
    v_recv,
    x_send,
    x_recv,
    y_send,
    y_recv,
    a_send,
    a_recv,
    up_send,
    down_send,
    far_send,
    d_recv,
    p_send,
    p_recv,
    z_send,
    z_recv,
    g_send,
    g_recv,
    t_send,
    t_recv,
):
    g, s, core, plane, zh = place()
    ahead = lax.rem(s + 1, 64)
    back = lax.rem(s + 63, 64)
    adjoint = g == 3
    direct = g < 3
    middle = (g == 1) | (g == 2)
    z = zh * 4 + g
    last = (plane == 15) & (core == 1)
    first = (plane == 0) & (core == 0)
    edge = last | first

    def at(depth, position, side):
        depth = lax.rem(depth, 8)
        return lax.rem(depth, 4), slab_of(lax.div(depth, 4), position, side)

    def peer16(d):
        g2 = lax.rem(g + d // 4, 4)
        zh2 = lax.rem(zh + (d // 2) % 2, 2)
        c2 = lax.rem(core + d % 2, 2)
        return g2, slab_of(zh2, plane, c2)

    def plane_peer(d):
        return lax.rem(plane + d, 16)

    barrier = pltpu.get_barrier_semaphore()

    def greet(device):
        pl.semaphore_signal(barrier, inc=1, device_id=device, device_id_type=MESH)

    greet((g, ahead))
    greet((g, back))
    for d in range(1, 16):
        greet((g, slab_of(zh, plane_peer(d), core)))
        greet(peer16(d))

    far_end = at(z + 4, 15 * (1 - core), 1 - core)
    greet(far_end)

    @pl.when(edge)
    def _():
        def one(i, carry):
            greet(at(z + 4, i, 1 - core))
            return carry

        lax.fori_loop(0, 16, one, 0)

    pl.semaphore_wait(barrier, 33 + jnp.where(edge, 16, 0))

    flow = [
        remote(v_ref, vleft, v_send.at[0], v_recv.at[0], (g, ahead)),
        remote(v_ref, vright, v_send.at[1], v_recv.at[1], (g, back)),
    ]
    for copy in flow:
        copy.start()

    def rows(c):
        return pl.ds(c * PER, PER)

    def halo(c):
        return [
            remote(u_ref.at[rows(c)], left.at[rows(c)], h_send.at[0, c], h_recv.at[0, c], (g, ahead)),
            remote(u_ref.at[rows(c)], right.at[rows(c)], h_send.at[1, c], h_recv.at[1, c], (g, back)),
        ]

    def half(i):
        return pl.ds(i * 8, 8)

    def to_relay(i):
        return remote(u_ref.at[half(i)], relay_buf, x_send.at[i], y_recv, (g, slab_of(zh, i, core)))

    def across(src, i, send_sem):
        return (
            remote(src, right.at[half(i)], send_sem, x_recv.at[i], far_end),
            remote(src, left.at[half(i)], send_sem, x_recv.at[i], far_end),
        )

    def start_across(src, i, send_sem):
        to_right, to_left = across(src, i, send_sem)

        @pl.when(core == 0)
        def _():
            to_right.start()

        @pl.when(core == 1)
        def _():
            to_left.start()

    @pl.when(edge)
    def _():
        def one(i, carry):
            @pl.when(i != plane)
            def _():
                to_relay(i).start()

            @pl.when(i == plane)
            def _():
                start_across(u_ref.at[half(i)], i, x_send.at[i])

            return carry

        lax.fori_loop(0, 16, one, 0)

    def start_halo(c, carry):
        ahead_copy, back_copy = halo(c)

        @pl.when(jnp.logical_not(last))
        def _():
            ahead_copy.start()

        @pl.when(jnp.logical_not(first))
        def _():
            back_copy.start()

        return carry

    lax.fori_loop(0, CHUNKS, start_halo, 0)

    def pass_on():
        pltpu.make_async_copy(relay_buf, relay_buf, y_recv).wait()
        start_across(relay_buf, plane, y_send)

    def halo_in(c):
        ahead_copy, back_copy = halo(c)

        @pl.when(jnp.logical_not(first))
        def _():
            ahead_copy.wait_recv()

        @pl.when(jnp.logical_not(last))
        def _():
            back_copy.wait_recv()

        @pl.when(edge)
        def _():
            for i in range(2):
                across(relay_buf, 2 * c + i, y_send)[0].wait_recv()

    for copy in flow:
        copy.wait()

    v = [vleft[k] for k in range(4)] + [v_ref[k] for k in range(4)] + [vright[k] for k in range(4)]
    for k in range(10):
        cp[k] = jnp.where(adjoint, diffuse_x + 0.5 * v[k + 2], diffuse_x - 0.5 * v[k + 1])
        cm[k] = jnp.where(adjoint, diffuse_x - 0.5 * v[k], diffuse_x + 0.5 * v[k + 1])

    def sections(snap, base):
        cells = [ref[snap, k].astype(jnp.float32) for ref in (left, u_ref, right) for k in range(4)]
        for section in range(SECTIONS):
            new = []
            for k in range(0, len(cells) - 2, 2):
                pair = jnp.concatenate([cells[k + 1], cells[k + 2]], axis=0).astype(jnp.bfloat16)
                lanes = (pltpu.roll(pair, 1, 1) + pltpu.roll(pair, 127, 1)).astype(jnp.float32)
                for j in range(2):
                    center = cells[k + 1 + j]
                    side = pltpu.roll(center, 1, 0) + pltpu.roll(center, 7, 0) + lanes[8 * j : 8 * j + 8]
                    new.append(
                        keep_center * center
                        + cp[section + k + j] * cells[k + j + 2]
                        + cm[section + k + j] * cells[k + j]
                        + diffuse_side * side
                    )
            cells = new
        for k in range(4):
            stage[pl.ds(base + k * 64, 8, stride=8), :] = cells[k]

    def chain(c):
        return remote(adj_ref.at[c], adj_ref.at[c], a_send.at[c], a_recv.at[c], (lax.max(g - 1, 0), s))

    def relay(c):
        @pl.when(middle)
        def _():
            chain(c).wait_recv()
            chain(c).start()

    def up(c):
        k = lax.min(g, 2)
        return remote(fields.at[k, c], fields.at[k, c], up_send.at[c], d_recv.at[k, c], (lax.min(g + 1, 3), s))

    def down(c):
        k = lax.min(g, 2)
        return remote(fields.at[k, c], fields.at[k, c], down_send.at[c], d_recv.at[k, c], (lax.max(g - 1, 0), s))

    def far(c):
        k = lax.max(lax.min(g - 1, 2), 0)
        return remote(fields.at[k, c], fields.at[k, c], far_send.at[c], d_recv.at[k, c], (lax.min(g + 1, 3), s))

    def chunk(c, carry):
        @pl.when(jnp.logical_not(edge) & (c == lax.div(plane + 2, 4)))
        def _():
            pass_on()

        halo_in(c)

        def one(part_no, inner):
            for i in range(8):
                sections(c * PER + part_no * 8 + i, part_no * 256 + i)
            return inner

        lax.fori_loop(0, 2, one, 0)

        def packed(q):
            low = stage[q * 8 : q * 8 + 8, :]
            high = stage[256 + q * 8 : 256 + q * 8 + 8, :]
            return jnp.concatenate([low, high], axis=0).astype(jnp.bfloat16)

        @pl.when(adjoint)
        def _():
            for q in range(32):
                adj_ref[c, q] = packed(q)
            chain(c).start()

        @pl.when(direct)
        def _():
            for q in range(32):
                fields[lax.min(g, 2), c, q] = packed(q)

            def start_up():
                for i in range(2):
                    up(2 * (c - CHUNKS + 4) + i).start()

            pl.when(c >= CHUNKS - 4)(start_up)

        @pl.when(c >= 1)
        def _():
            relay(c - 1)

        return carry

    lax.fori_loop(0, CHUNKS, chunk, 0)
    relay(CHUNKS - 1)

    def spread_fields(begin, end):
        @pl.when(middle)
        def _():
            def one(c, carry):
                down(c).start()
                far(c).wait_recv()
                far(c).start()
                return carry

            lax.fori_loop(begin, end, one, 0)

    @pl.when(g == 0)
    def _():
        def one(c, carry):
            chain(c).wait_recv()
            return carry

        lax.fori_loop(0, CHUNKS, one, 0)

    spread_fields(0, EARLY)

    def scatter(d):
        p2 = plane_peer(d)
        return remote(part.at[p2], rs_buf.at[plane], p_send.at[p2], p_recv.at[plane], (g, slab_of(zh, p2, core)))

    def scatter_in(d):
        p2 = plane_peer(d)
        return remote(part.at[plane], rs_buf.at[p2], p_send.at[plane], p_recv.at[p2], (g, slab_of(zh, p2, core)))

    slot = g * 4 + zh * 2 + core
    own_slot = lax.min(slot, 11)

    def spread(d):
        return remote(tile, zbuf.at[own_slot], z_send.at[d], z_recv.at[own_slot], peer16(d))

    @pl.when(direct)
    def _():
        here = lax.min(g, 2)

        def product(q, total):
            lhs = [adj_ref[:, 2 * q + j].reshape(SNAP, 128) for j in range(2)]
            rhs = [fields[here, :, 2 * q + j].reshape(SNAP, 128) for j in range(2)]
            return total + lax.dot_general(
                jnp.concatenate(lhs, axis=1),
                jnp.concatenate(rhs, axis=1),
                (((1,), (1,)), ((), ())),
                preferred_element_type=jnp.float32,
            )

        total = lax.fori_loop(0, 16, product, jnp.zeros((SNAP, SNAP), jnp.float32))
        part[...] = total.reshape(16, 8, SNAP)
        for d in range(1, 16):
            scatter(d).start()
        rs_buf[plane] = part[plane]
        for d in range(1, 16):
            scatter_in(d).wait_recv()
        tile[...] = jnp.sum(rs_buf[...], axis=0)
        for d in range(1, 16):
            spread(d).start()
        zbuf[own_slot] = tile[...]

    spread_fields(EARLY, CHUNKS)

    for here in range(12):

        @pl.when(slot != here)
        def _():
            pltpu.make_async_copy(zbuf.at[here], zbuf.at[here], z_recv.at[here]).wait()

    for k in range(3):
        mine[k] = jnp.sum(zbuf[k * 4 : k * 4 + 4], axis=0) * scale

    def share(d):
        p2 = plane_peer(d)
        return remote(mine, coup_ref.at[plane], g_send.at[p2], g_recv.at[plane], (g, slab_of(zh, p2, core)))

    def share_in(d):
        p2 = plane_peer(d)
        return remote(mine, coup_ref.at[p2], g_send.at[plane], g_recv.at[p2], (g, slab_of(zh, p2, core)))

    for d in range(1, 16):
        share(d).start()
    coup_ref[plane] = mine[...]
    for d in range(1, 16):
        share_in(d).wait_recv()

    root = invert(coup_ref, m_ref)

    def weights(row, k):
        return (
            jnp.dot(
                m_ref[pl.ds(pl.multiple_of(row, 32), 32), :],
                coup_ref[:, k].reshape(SNAP, SNAP),
                precision=lax.Precision.HIGHEST,
                preferred_element_type=jnp.float32,
            )
            / root
        ).astype(jnp.bfloat16)

    def times(w, ref, q):
        rhs = jnp.concatenate([ref[:, 2 * q + j].reshape(SNAP, 128) for j in range(2)], axis=1)
        out = jnp.dot(w, rhs, preferred_element_type=jnp.float32)
        return [out[:, j * 128 : j * 128 + 128] for j in range(2)]

    def arrived(k):
        def one(c, carry):
            pltpu.make_async_copy(fields.at[k, c], fields.at[k, c], d_recv.at[k, c]).wait()
            return carry

        lax.fori_loop(0, CHUNKS, one, 0)

    def post(i):
        to = jnp.where(g == 1, 0, 3)
        block = pl.ds(i * 8, 8)
        return remote(terms.at[block], inbox.at[block], t_send.at[i], t_recv.at[i], (to, s))

    for holder, k, row in ((1, 2, 0), (2, 0, 96)):

        @pl.when(g == holder)
        def _():
            arrived(k)
            w = weights(row, k)
            for i in range(4):

                def one(q, carry):
                    for j, x in enumerate(times(w, fields.at[k], q)):
                        terms[2 * q + j] = x.astype(jnp.bfloat16)
                    return carry

                lax.fori_loop(i * 4, i * 4 + 4, one, 0)
                post(i).start()

    own_inverse = m_ref[pl.ds(pl.multiple_of(g * 32, 32), 32), :].astype(jnp.bfloat16)

    def adjoint_modes(q, carry):
        for j, x in enumerate(times(own_inverse, adj_ref, q)):
            am_ref[2 * q + j] = x.astype(jnp.bfloat16)
        return carry

    lax.fori_loop(0, 16, adjoint_modes, 0)

    @pl.when((g == 0) | adjoint)
    def _():
        arrived(1)

    @pl.when(adjoint)
    def _():
        arrived(2)

    w1 = weights(g * 32, 1)

    def one_group(q, carry):
        for j, x in enumerate(times(w1, fields.at[1], q)):
            acc[2 * q + j] = x
        return carry

    lax.fori_loop(0, 16, one_group, 0)
    for k, present in ((0, direct), (2, g > 0)):

        @pl.when(present)
        def _():
            w = weights(g * 32, k)

            def add(q, carry):
                for j, x in enumerate(times(w, fields.at[k], q)):
                    acc[2 * q + j] += x
                return carry

            lax.fori_loop(0, 16, add, 0)

    @pl.when(middle)
    def _():
        def out(q, carry):
            dm_ref[q] = acc[q].astype(jnp.bfloat16)
            return carry

        lax.fori_loop(0, 32, out, 0)

    @pl.when(jnp.logical_not(middle))
    def _():
        for i in range(4):
            block = pl.ds(i * 8, 8)
            pltpu.make_async_copy(inbox.at[block], inbox.at[block], t_recv.at[i]).wait()

            def out(q, carry):
                dm_ref[q] = (acc[q] + inbox[q].astype(jnp.float32)).astype(jnp.bfloat16)
                return carry

            lax.fori_loop(i * 8, i * 8 + 8, out, 0)

    def drain(c, carry):
        ahead_copy, back_copy = halo(c)

        @pl.when(jnp.logical_not(last))
        def _():
            ahead_copy.wait_send()

        @pl.when(jnp.logical_not(first))
        def _():
            back_copy.wait_send()

        @pl.when(g > 0)
        def _():
            chain(c).wait_send()

        @pl.when(direct)
        def _():
            up(c).wait_send()

        @pl.when(middle)
        def _():
            down(c).wait_send()
            far(c).wait_send()

        return carry

    lax.fori_loop(0, CHUNKS, drain, 0)

    @pl.when(edge)
    def _():
        def one(i, carry):
            to_relay(i).wait_send()
            return carry

        lax.fori_loop(0, 16, one, 0)

    @pl.when(jnp.logical_not(edge))
    def _():
        across(relay_buf, plane, y_send)[0].wait_send()

    for d in range(1, 16):
        share(d).wait_send()

    @pl.when(direct)
    def _():
        for d in range(1, 16):
            scatter(d).wait_send()
            spread(d).wait_send()

    @pl.when(middle)
    def _():
        for i in range(4):
            post(i).wait_send()


def invert(coup_ref, m_ref):
    gram = jnp.zeros((SNAP, SNAP), jnp.float32)
    for k in range(3):
        c = coup_ref[:, k].reshape(SNAP, SNAP)
        gram = gram + lax.dot_general(
            c, c, (((1,), (1,)), ((), ())), precision=lax.Precision.HIGHEST, preferred_element_type=jnp.float32
        )
    row = lax.broadcasted_iota(jnp.int32, (SNAP, SNAP), 0)
    col = lax.broadcasted_iota(jnp.int32, (SNAP, SNAP), 1)
    eye = (row == col).astype(jnp.float32)
    energy = jnp.sum(gram * eye, axis=(0, 1), keepdims=True) / SNAP
    m_ref[...] = gram / energy + damping * eye

    sub = lax.broadcasted_iota(jnp.int32, (8, SNAP), 0)
    lane = lax.broadcasted_iota(jnp.int32, (8, SNAP), 1)

    def spread_row(x, j):
        return jnp.broadcast_to(x[j : j + 1, :], (8, SNAP))

    for b in range(16):
        full = m_ref[...]
        columns = [jnp.broadcast_to(full[:, 8 * b + j : 8 * b + j + 1], (SNAP, SNAP)) for j in range(8)]
        panel = full[8 * b : 8 * b + 8, :]
        pivots = [c[8 * b : 8 * b + 8, :] for c in columns]
        for j in range(8):
            own = sub == j
            inv = 1.0 / spread_row(pivots[j], j)
            pj = pivots[j]
            panel = jnp.where(lane == 8 * b + j, own.astype(jnp.float32), panel)
            new = spread_row(panel, j) * inv
            panel = jnp.where(own, new, panel - pj * new)
            for i in range(j + 1, 8):
                new = spread_row(pivots[i], j) * inv
                pivots[i] = jnp.where(own, new, pivots[i] - pj * new)
        inside = (lane >= 8 * b) & (lane < 8 * b + 8)
        spread = [spread_row(panel, j) for j in range(8)]
        for t in range(16):
            if t == b:
                m_ref[8 * t : 8 * t + 8, :] = panel
            else:
                rest = jnp.where(inside, 0.0, full[8 * t : 8 * t + 8, :])
                for j in range(8):
                    rest = rest - columns[j][8 * t : 8 * t + 8, :] * spread[j]
                m_ref[8 * t : 8 * t + 8, :] = rest
    return jnp.sqrt(energy)


def per_device(snapshots, base_flow):
    field = snapshots[0]
    f32, bf16 = jnp.float32, jnp.bfloat16
    vmem = pl.BlockSpec(memory_space=pltpu.VMEM)
    dma = pltpu.SemaphoreType.DMA
    slab_shape = field.shape
    cells = 64 * math.prod(slab_shape[1:])
    scale = 1.0 / math.sqrt(cells)
    modes = jax.ShapeDtypeStruct((32, 32, 128), bf16)
    dm, am = pl.pallas_call(
        functools.partial(kernel, scale),
        out_shape=(modes, modes),
        in_specs=[vmem] * 2,
        out_specs=(vmem,) * 2,
        scratch_shapes=[
            pltpu.VMEM(slab_shape, bf16),
            pltpu.VMEM(slab_shape, bf16),
            pltpu.VMEM((8,) + slab_shape[1:], bf16),
            pltpu.VMEM((4, 8, 128), f32),
            pltpu.VMEM((4, 8, 128), f32),
            pltpu.VMEM((10, 8, 128), f32),
            pltpu.VMEM((10, 8, 128), f32),
            pltpu.VMEM((512, 128), f32),
            pltpu.VMEM((3, CHUNKS, 32, PER, 128), bf16),
            pltpu.VMEM((CHUNKS, 32, PER, 128), bf16),
            pltpu.VMEM((16, 8, SNAP), f32),
            pltpu.VMEM((16, 8, SNAP), f32),
            pltpu.VMEM((8, SNAP), f32),
            pltpu.VMEM((12, 8, SNAP), f32),
            pltpu.VMEM((3, 8, SNAP), f32),
            pltpu.VMEM((16, 3, 8, SNAP), f32),
            pltpu.VMEM((SNAP, SNAP), f32),
            pltpu.VMEM((32, 32, 128), f32),
            pltpu.VMEM((32, 32, 128), bf16),
            pltpu.VMEM((32, 32, 128), bf16),
            dma((2, CHUNKS)),
            dma((2, CHUNKS)),
            dma((2,)),
            dma((2,)),
            dma((16,)),
            dma((16,)),
            dma,
            dma,
            dma((CHUNKS,)),
            dma((CHUNKS,)),
            dma((CHUNKS,)),
            dma((CHUNKS,)),
            dma((CHUNKS,)),
            dma((3, CHUNKS)),
            dma((16,)),
            dma((16,)),
            dma((16,)),
            dma((12,)),
            dma((16,)),
            dma((16,)),
            dma((4,)),
            dma((4,)),
        ],
        compiler_params=pltpu.CompilerParams(
            collective_id=0, has_side_effects=True, vmem_limit_bytes=48 * MIB
        ),
        name="pod",
    )(field, base_flow)

    def placed(x):
        return x.reshape(4, 8, 32, 128).transpose(2, 0, 1, 3)

    return placed(dm), placed(am)


def solution(mesh):
    return jax.shard_map(
        per_device,
        mesh=mesh,
        in_specs=(P("grp", None, "slab", None, None), P("slab", None, None)),
        out_specs=(P("grp", "slab", None, None), P("grp", "slab", None, None)),
        check_vma=False,
    )
```

time: 128 us -> 97.8 us (0.76)
  the two profiles are of different devices: /device:TPU:64 before, /device:TPU:72 now
where the time goes in v2:
time: 97.8 us; the launch traced here: 97.6 us
  Pallas kernels  94.1 us (96%)
  local copies, waits for them, and re-layouts  2.93 us (3%)
    pallas_call x1, Pallas kernels, per_device(): pl.pallas_call(functools.partial(kernel, scale), out_shape=(modes, modes)...  94.1 us

profile of v2, /device:TPU:72, one launch (start us, length us, event | category | flops | bytes accessed | tf_op | source)
XLA Modules:
  0.0 97.6 jit_solution(1544457565620741870)
XLA Ops:
  0.6 0.0 copy-start
  0.6 1.2 %copy-done = bf16[1,128,4,8,128]{4,3,2,1,0:T(8,128)(2,1)S(1)} copy-done((bf16[1,128,4,8,128]{4,3,2,1,0:T(8,128)(2,1)S(1)}, bf16[1,128,4,8,128]{4,3,2,1,0:T(8,128)(2,1)}, u32[]{:S(2)}) %copy-start) | copy-done | bytes 1048600
  1.9 0.0 copy-start.1
  1.9 0.7 copy-done.1
  2.6 94.1 %pod.1 = (bf16[32,32,128]{2,1,0:T(8,128)(2,1)S(1)}, bf16[32,32,128]{2,1,0:T(8,128)(2,1)S(1)}) custom-call(bf16[128,4,8,128]{3,2,1,0:T(8,128)(2,1)S(1)} %bitcast.7, f32[4,8,128]{2,1,0:T(8,128)S(1)} %copy-done.1), custom_call_target="tpu_custom_call" | custom-call | tf_op jit(solution)/shard_map/pod/pallas_call | solution.py:625
  96.6 1.0 %copy_bitcast_fusion = (bf16[32,4,8,128]{3,2,1,0:T(8,128)(2,1)}, bf16[32,4,8,128]{3,2,1,0:T(8,128)(2,1)}) fusion(bf16[4,8,32,128]{3,2,1,0:T(8,128)(2,1)S(1)} %bitcast.9, bf16[4,8,32,128]{3,2,1,0:T(8,128)(2,1)S(1)} %bitcast.8), kind=kLoop, calls=%fused_computation | loop fusion | bytes 1048576 | tf_op jit(solution)/shard_map/transpose | solution.py:681
Async XLA Ops:
  0.6 1.2 %copy-start = (bf16[1,128,4,8,128]{4,3,2,1,0:T(8,128)(2,1)S(1)}, bf16[1,128,4,8,128]{4,3,2,1,0:T(8,128)(2,1)}, u32[]{:S(2)}) copy-start(bf16[1,128,4,8,128]{4,3,2,1,0:T(8,128)(2,1)} %param.2) | copy-start | bytes 3145732
  1.9 0.7 copy-start.1

commit v3 on v2

--- a/solution.py
+++ b/solution.py
@@ -14,7 +14,6 @@
 PER = SNAP // CHUNKS
 MESH = pl.DeviceIdType.MESH
 MIB = 1 << 20
-EARLY = 2
 
 diffuse_x = 0.35
 diffuse_side = 0.05
@@ -55,8 +54,8 @@
     cp,
     cm,
     stage,
-    fields,
-    adj_ref,
+    own,
+    quart,
     part,
     rs_buf,
     tile,
@@ -64,9 +63,8 @@
     mine,
     coup_ref,
     m_ref,
-    acc,
+    wide,
     terms,
-    inbox,
     h_send,
     h_recv,
     v_send,
@@ -75,27 +73,21 @@
     x_recv,
     y_send,
     y_recv,
-    a_send,
-    a_recv,
-    up_send,
-    down_send,
-    far_send,
-    d_recv,
+    q_send,
+    q_recv,
     p_send,
     p_recv,
     z_send,
     z_recv,
     g_send,
     g_recv,
-    t_send,
-    t_recv,
+    o_send,
+    o_recv,
 ):
     g, s, core, plane, zh = place()
     ahead = lax.rem(s + 1, 64)
     back = lax.rem(s + 63, 64)
     adjoint = g == 3
-    direct = g < 3
-    middle = (g == 1) | (g == 2)
     z = zh * 4 + g
     last = (plane == 15) & (core == 1)
     first = (plane == 0) & (core == 0)
@@ -255,29 +247,16 @@
         for k in range(4):
             stage[pl.ds(base + k * 64, 8, stride=8), :] = cells[k]
 
-    def chain(c):
-        return remote(adj_ref.at[c], adj_ref.at[c], a_send.at[c], a_recv.at[c], (lax.max(g - 1, 0), s))
-
-    def relay(c):
-        @pl.when(middle)
-        def _():
-            chain(c).wait_recv()
-            chain(c).start()
-
-    def up(c):
-        k = lax.min(g, 2)
-        return remote(fields.at[k, c], fields.at[k, c], up_send.at[c], d_recv.at[k, c], (lax.min(g + 1, 3), s))
-
-    def down(c):
-        k = lax.min(g, 2)
-        return remote(fields.at[k, c], fields.at[k, c], down_send.at[c], d_recv.at[k, c], (lax.max(g - 1, 0), s))
-
-    def far(c):
-        k = lax.max(lax.min(g - 1, 2), 0)
-        return remote(fields.at[k, c], fields.at[k, c], far_send.at[c], d_recv.at[k, c], (lax.min(g + 1, 3), s))
+    def piece(c, d):
+        r = lax.rem(g + d, 4)
+        return remote(own.at[c, r], quart.at[g, c], q_send.at[c, d], q_recv.at[g, c], (r, s))
+
+    def piece_in(c, d):
+        k = lax.rem(g + d, 4)
+        return remote(own.at[c, k], quart.at[k, c], q_send.at[c, d], q_recv.at[k, c], (k, s))
 
     def chunk(c, carry):
-        @pl.when(jnp.logical_not(edge) & (c == lax.div(plane + 2, 4)))
+        @pl.when(jnp.logical_not(edge) & (c == lax.div(plane + 2, 5)))
         def _():
             pass_on()
 
@@ -295,52 +274,21 @@
             high = stage[256 + q * 8 : 256 + q * 8 + 8, :]
             return jnp.concatenate([low, high], axis=0).astype(jnp.bfloat16)
 
-        @pl.when(adjoint)
-        def _():
-            for q in range(32):
-                adj_ref[c, q] = packed(q)
-            chain(c).start()
-
-        @pl.when(direct)
-        def _():
-            for q in range(32):
-                fields[lax.min(g, 2), c, q] = packed(q)
-
-            def start_up():
-                for i in range(2):
-                    up(2 * (c - CHUNKS + 4) + i).start()
-
-            pl.when(c >= CHUNKS - 4)(start_up)
-
-        @pl.when(c >= 1)
-        def _():
-            relay(c - 1)
-
+        for q in range(32):
+            own[c, q // 8, q % 8] = packed(q)
+        for d in range(1, 4):
+            piece(c, d).start()
+        quart[g, c] = own[c, g]
         return carry
 
     lax.fori_loop(0, CHUNKS, chunk, 0)
-    relay(CHUNKS - 1)
-
-    def spread_fields(begin, end):
-        @pl.when(middle)
-        def _():
-            def one(c, carry):
-                down(c).start()
-                far(c).wait_recv()
-                far(c).start()
-                return carry
-
-            lax.fori_loop(begin, end, one, 0)
-
-    @pl.when(g == 0)
-    def _():
-        def one(c, carry):
-            chain(c).wait_recv()
-            return carry
-
-        lax.fori_loop(0, CHUNKS, one, 0)
-
-    spread_fields(0, EARLY)
+
+    def gathered(c, carry):
+        for d in range(1, 4):
+            piece_in(c, d).wait_recv()
+        return carry
+
+    lax.fori_loop(0, CHUNKS, gathered, 0)
 
     def scatter(d):
         p2 = plane_peer(d)
@@ -351,47 +299,38 @@
         return remote(part.at[plane], rs_buf.at[p2], p_send.at[plane], p_recv.at[p2], (g, slab_of(zh, p2, core)))
 
     slot = g * 4 + zh * 2 + core
-    own_slot = lax.min(slot, 11)
 
     def spread(d):
-        return remote(tile, zbuf.at[own_slot], z_send.at[d], z_recv.at[own_slot], peer16(d))
-
-    @pl.when(direct)
-    def _():
-        here = lax.min(g, 2)
+        return remote(tile, zbuf.at[slot], z_send.at[d], z_recv.at[slot], peer16(d))
+
+    def pair(k, q):
+        return jnp.concatenate([quart[k, :, 2 * q + j].reshape(SNAP, 128) for j in range(2)], axis=1)
+
+    for k in range(3):
 
         def product(q, total):
-            lhs = [adj_ref[:, 2 * q + j].reshape(SNAP, 128) for j in range(2)]
-            rhs = [fields[here, :, 2 * q + j].reshape(SNAP, 128) for j in range(2)]
             return total + lax.dot_general(
-                jnp.concatenate(lhs, axis=1),
-                jnp.concatenate(rhs, axis=1),
-                (((1,), (1,)), ((), ())),
-                preferred_element_type=jnp.float32,
+                pair(3, q), pair(k, q), (((1,), (1,)), ((), ())), preferred_element_type=jnp.float32
             )
 
-        total = lax.fori_loop(0, 16, product, jnp.zeros((SNAP, SNAP), jnp.float32))
-        part[...] = total.reshape(16, 8, SNAP)
-        for d in range(1, 16):
-            scatter(d).start()
-        rs_buf[plane] = part[plane]
-        for d in range(1, 16):
-            scatter_in(d).wait_recv()
-        tile[...] = jnp.sum(rs_buf[...], axis=0)
-        for d in range(1, 16):
-            spread(d).start()
-        zbuf[own_slot] = tile[...]
-
-    spread_fields(EARLY, CHUNKS)
-
-    for here in range(12):
+        total = lax.fori_loop(0, 4, product, jnp.zeros((SNAP, SNAP), jnp.float32))
+        part[:, k] = total.reshape(16, 8, SNAP)
+    for d in range(1, 16):
+        scatter(d).start()
+    rs_buf[plane] = part[plane]
+    for d in range(1, 16):
+        scatter_in(d).wait_recv()
+    tile[...] = jnp.sum(rs_buf[...], axis=0)
+    for d in range(1, 16):
+        spread(d).start()
+    zbuf[slot] = tile[...]
+    for here in range(16):
 
         @pl.when(slot != here)
         def _():
             pltpu.make_async_copy(zbuf.at[here], zbuf.at[here], z_recv.at[here]).wait()
 
-    for k in range(3):
-        mine[k] = jnp.sum(zbuf[k * 4 : k * 4 + 4], axis=0) * scale
+    mine[...] = jnp.sum(zbuf[...], axis=0) * scale
 
     def share(d):
         p2 = plane_peer(d)
@@ -409,10 +348,37 @@
 
     root = invert(coup_ref, m_ref)
 
-    def weights(row, k):
-        return (
+    def post(d, kind):
+        r = lax.rem(g + d, 4)
+        out = (dm_ref, am_ref)[kind]
+        here = pl.ds(pl.multiple_of(g * 8, 8), 8)
+        return remote(terms.at[kind, r], out.at[here], o_send.at[kind, d], o_recv.at[kind, g], (r, s))
+
+    def post_in(d, kind):
+        k = lax.rem(g + d, 4)
+        out = (dm_ref, am_ref)[kind]
+        there = pl.ds(pl.multiple_of(k * 8, 8), 8)
+        return remote(terms.at[kind, k], out.at[there], o_send.at[kind, d], o_recv.at[kind, k], (k, s))
+
+    def modes(kind, value):
+        def one(q, carry):
+            x = value(q).astype(jnp.bfloat16)
+            for j in range(2):
+                terms[kind, :, 2 * q + j] = x[:, j * 128 : j * 128 + 128].reshape(4, 32, 128)
+            return carry
+
+        lax.fori_loop(0, 4, one, 0)
+        for d in (2, 3, 1):
+            post(d, kind).start()
+        here = pl.ds(pl.multiple_of(g * 8, 8), 8)
+        (dm_ref, am_ref)[kind][here] = terms[kind, g]
+
+    inverse = m_ref[...].astype(jnp.bfloat16)
+    modes(1, lambda q: jnp.dot(inverse, pair(3, q), preferred_element_type=jnp.float32))
+    for k in range(3):
+        wide[k] = (
             jnp.dot(
-                m_ref[pl.ds(pl.multiple_of(row, 32), 32), :],
+                m_ref[...],
                 coup_ref[:, k].reshape(SNAP, SNAP),
                 precision=lax.Precision.HIGHEST,
                 preferred_element_type=jnp.float32,
@@ -420,96 +386,16 @@
             / root
         ).astype(jnp.bfloat16)
 
-    def times(w, ref, q):
-        rhs = jnp.concatenate([ref[:, 2 * q + j].reshape(SNAP, 128) for j in range(2)], axis=1)
-        out = jnp.dot(w, rhs, preferred_element_type=jnp.float32)
-        return [out[:, j * 128 : j * 128 + 128] for j in range(2)]
-
-    def arrived(k):
-        def one(c, carry):
-            pltpu.make_async_copy(fields.at[k, c], fields.at[k, c], d_recv.at[k, c]).wait()
-            return carry
-
-        lax.fori_loop(0, CHUNKS, one, 0)
-
-    def post(i):
-        to = jnp.where(g == 1, 0, 3)
-        block = pl.ds(i * 8, 8)
-        return remote(terms.at[block], inbox.at[block], t_send.at[i], t_recv.at[i], (to, s))
-
-    for holder, k, row in ((1, 2, 0), (2, 0, 96)):
-
-        @pl.when(g == holder)
-        def _():
-            arrived(k)
-            w = weights(row, k)
-            for i in range(4):
-
-                def one(q, carry):
-                    for j, x in enumerate(times(w, fields.at[k], q)):
-                        terms[2 * q + j] = x.astype(jnp.bfloat16)
-                    return carry
-
-                lax.fori_loop(i * 4, i * 4 + 4, one, 0)
-                post(i).start()
-
-    own_inverse = m_ref[pl.ds(pl.multiple_of(g * 32, 32), 32), :].astype(jnp.bfloat16)
-
-    def adjoint_modes(q, carry):
-        for j, x in enumerate(times(own_inverse, adj_ref, q)):
-            am_ref[2 * q + j] = x.astype(jnp.bfloat16)
-        return carry
-
-    lax.fori_loop(0, 16, adjoint_modes, 0)
-
-    @pl.when((g == 0) | adjoint)
-    def _():
-        arrived(1)
-
-    @pl.when(adjoint)
-    def _():
-        arrived(2)
-
-    w1 = weights(g * 32, 1)
-
-    def one_group(q, carry):
-        for j, x in enumerate(times(w1, fields.at[1], q)):
-            acc[2 * q + j] = x
-        return carry
-
-    lax.fori_loop(0, 16, one_group, 0)
-    for k, present in ((0, direct), (2, g > 0)):
-
-        @pl.when(present)
-        def _():
-            w = weights(g * 32, k)
-
-            def add(q, carry):
-                for j, x in enumerate(times(w, fields.at[k], q)):
-                    acc[2 * q + j] += x
-                return carry
-
-            lax.fori_loop(0, 16, add, 0)
-
-    @pl.when(middle)
-    def _():
-        def out(q, carry):
-            dm_ref[q] = acc[q].astype(jnp.bfloat16)
-            return carry
-
-        lax.fori_loop(0, 32, out, 0)
-
-    @pl.when(jnp.logical_not(middle))
-    def _():
-        for i in range(4):
-            block = pl.ds(i * 8, 8)
-            pltpu.make_async_copy(inbox.at[block], inbox.at[block], t_recv.at[i]).wait()
-
-            def out(q, carry):
-                dm_ref[q] = (acc[q] + inbox[q].astype(jnp.float32)).astype(jnp.bfloat16)
-                return carry
-
-            lax.fori_loop(i * 8, i * 8 + 8, out, 0)
+    def direct_value(q):
+        total = jnp.dot(wide[0], pair(0, q), preferred_element_type=jnp.float32)
+        for k in (1, 2):
+            total = total + jnp.dot(wide[k], pair(k, q), preferred_element_type=jnp.float32)
+        return total
+
+    modes(0, direct_value)
+    for kind in (1, 0):
+        for d in range(1, 4):
+            post_in(d, kind).wait_recv()
 
     def drain(c, carry):
         ahead_copy, back_copy = halo(c)
@@ -522,19 +408,8 @@
         def _():
             back_copy.wait_send()
 
-        @pl.when(g > 0)
-        def _():
-            chain(c).wait_send()
-
-        @pl.when(direct)
-        def _():
-            up(c).wait_send()
-
-        @pl.when(middle)
-        def _():
-            down(c).wait_send()
-            far(c).wait_send()
-
+        for d in range(1, 4):
+            piece(c, d).wait_send()
         return carry
 
     lax.fori_loop(0, CHUNKS, drain, 0)
@@ -552,18 +427,12 @@
         across(relay_buf, plane, y_send)[0].wait_send()
 
     for d in range(1, 16):
+        scatter(d).wait_send()
+        spread(d).wait_send()
         share(d).wait_send()
-
-    @pl.when(direct)
-    def _():
-        for d in range(1, 16):
-            scatter(d).wait_send()
-            spread(d).wait_send()
-
-    @pl.when(middle)
-    def _():
-        for i in range(4):
-            post(i).wait_send()
+    for kind in range(2):
+        for d in range(1, 4):
+            post(d, kind).wait_send()
 
 
 def invert(coup_ref, m_ref):
@@ -636,18 +505,17 @@
             pltpu.VMEM((10, 8, 128), f32),
             pltpu.VMEM((10, 8, 128), f32),
             pltpu.VMEM((512, 128), f32),
-            pltpu.VMEM((3, CHUNKS, 32, PER, 128), bf16),
-            pltpu.VMEM((CHUNKS, 32, PER, 128), bf16),
-            pltpu.VMEM((16, 8, SNAP), f32),
-            pltpu.VMEM((16, 8, SNAP), f32),
-            pltpu.VMEM((8, SNAP), f32),
-            pltpu.VMEM((12, 8, SNAP), f32),
+            pltpu.VMEM((CHUNKS, 4, 8, PER, 128), bf16),
+            pltpu.VMEM((4, CHUNKS, 8, PER, 128), bf16),
+            pltpu.VMEM((16, 3, 8, SNAP), f32),
+            pltpu.VMEM((16, 3, 8, SNAP), f32),
+            pltpu.VMEM((3, 8, SNAP), f32),
+            pltpu.VMEM((16, 3, 8, SNAP), f32),
             pltpu.VMEM((3, 8, SNAP), f32),
             pltpu.VMEM((16, 3, 8, SNAP), f32),
             pltpu.VMEM((SNAP, SNAP), f32),
-            pltpu.VMEM((32, 32, 128), f32),
-            pltpu.VMEM((32, 32, 128), bf16),
-            pltpu.VMEM((32, 32, 128), bf16),
+            pltpu.VMEM((3, SNAP, SNAP), bf16),
+            pltpu.VMEM((2, 4, 8, 32, 128), bf16),
             dma((2, CHUNKS)),
             dma((2, CHUNKS)),
             dma((2,)),
@@ -656,20 +524,16 @@
             dma((16,)),
             dma,
             dma,
-            dma((CHUNKS,)),
-            dma((CHUNKS,)),
-            dma((CHUNKS,)),
-            dma((CHUNKS,)),
-            dma((CHUNKS,)),
-            dma((3, CHUNKS)),
-            dma((16,)),
-            dma((16,)),
-            dma((16,)),
-            dma((12,)),
-            dma((16,)),
-            dma((16,)),
-            dma((4,)),
-            dma((4,)),
+            dma((CHUNKS, 4)),
+            dma((4, CHUNKS)),
+            dma((16,)),
+            dma((16,)),
+            dma((16,)),
+            dma((16,)),
+            dma((16,)),
+            dma((16,)),
+            dma((2, 4)),
+            dma((2, 4)),
         ],
         compiler_params=pltpu.CompilerParams(
             collective_id=0, has_side_effects=True, vmem_limit_bytes=48 * MIB

time: 97.8 us -> 84.8 us (0.87)
  the two profiles are of different devices: /device:TPU:72 before, /device:TPU:64 now
where the time goes in v3:
time: 84.8 us; the launch traced here: 84 us
  Pallas kernels  80.4 us (95%)
  local copies, waits for them, and re-layouts  2.93 us (3%)
    pallas_call x1, Pallas kernels, per_device(): pl.pallas_call(functools.partial(kernel, scale), out_shape=(modes, modes)...  80.4 us
    unnamed x4, local copies, waits for them, and re-layouts  1.93 us

profile of v3, /device:TPU:64, one launch (start us, length us, event | category | flops | bytes accessed | tf_op | source)
XLA Modules:
  0.0 84.0 jit_solution(14622998507083936240)
XLA Ops:
  0.6 0.0 copy-start
  0.6 1.2 %copy-done = bf16[1,128,4,8,128]{4,3,2,1,0:T(8,128)(2,1)S(1)} copy-done((bf16[1,128,4,8,128]{4,3,2,1,0:T(8,128)(2,1)S(1)}, bf16[1,128,4,8,128]{4,3,2,1,0:T(8,128)(2,1)}, u32[]{:S(2)}) %copy-start) | copy-done | bytes 1048600
  1.9 0.0 copy-start.1
  1.9 0.7 copy-done.1
  2.6 80.4 %pod.1 = (bf16[32,32,128]{2,1,0:T(8,128)(2,1)S(1)}, bf16[32,32,128]{2,1,0:T(8,128)(2,1)S(1)}) custom-call(bf16[128,4,8,128]{3,2,1,0:T(8,128)(2,1)S(1)} %bitcast.7, f32[4,8,128]{2,1,0:T(8,128)S(1)} %copy-done.1), custom_call_target="tpu_custom_call" | custom-call | tf_op jit(solution)/shard_map/pod/pallas_call | solution.py:494
  83.0 1.0 %copy_bitcast_fusion = (bf16[32,4,8,128]{3,2,1,0:T(8,128)(2,1)}, bf16[32,4,8,128]{3,2,1,0:T(8,128)(2,1)}) fusion(bf16[4,8,32,128]{3,2,1,0:T(8,128)(2,1)S(1)} %bitcast.9, bf16[4,8,32,128]{3,2,1,0:T(8,128)(2,1)S(1)} %bitcast.8), kind=kLoop, calls=%fused_computation | loop fusion | bytes 1048576 | tf_op jit(solution)/shard_map/transpose | solution.py:545
Async XLA Ops:
  0.6 1.2 %copy-start = (bf16[1,128,4,8,128]{4,3,2,1,0:T(8,128)(2,1)S(1)}, bf16[1,128,4,8,128]{4,3,2,1,0:T(8,128)(2,1)}, u32[]{:S(2)}) copy-start(bf16[1,128,4,8,128]{4,3,2,1,0:T(8,128)(2,1)} %param.2) | copy-start | bytes 3145732
  1.9 0.7 copy-start.1

commit v4 on v3

--- a/solution.py
+++ b/solution.py
@@ -42,10 +42,12 @@
 
 def kernel(
     scale,
+    u_hbm,
+    v_hbm,
+    dm_ref,
+    am_ref,
     u_ref,
     v_ref,
-    dm_ref,
-    am_ref,
     left,
     right,
     relay_buf,
@@ -57,6 +59,7 @@
     own,
     quart,
     part,
+    pair_buf,
     rs_buf,
     tile,
     zbuf,
@@ -65,6 +68,9 @@
     m_ref,
     wide,
     terms,
+    in_sem,
+    c_send,
+    c_recv,
     h_send,
     h_recv,
     v_send,
@@ -97,15 +103,17 @@
         depth = lax.rem(depth, 8)
         return lax.rem(depth, 4), slab_of(lax.div(depth, 4), position, side)
 
-    def peer16(d):
-        g2 = lax.rem(g + d // 4, 4)
-        zh2 = lax.rem(zh + (d // 2) % 2, 2)
-        c2 = lax.rem(core + d % 2, 2)
-        return g2, slab_of(zh2, plane, c2)
-
     def plane_peer(d):
         return lax.rem(plane + d, 16)
 
+    owner = lax.div(plane, 8) == core
+    partner = (g, slab_of(zh, plane, 1 - core))
+    loads = [
+        pltpu.make_async_copy(v_hbm, v_ref, in_sem.at[0]),
+        pltpu.make_async_copy(u_hbm, u_ref, in_sem.at[1]),
+    ]
+    for load in loads:
+        load.start()
     barrier = pltpu.get_barrier_semaphore()
 
     def greet(device):
@@ -113,10 +121,12 @@
 
     greet((g, ahead))
     greet((g, back))
+    greet(partner)
     for d in range(1, 16):
-        greet((g, slab_of(zh, plane_peer(d), core)))
-        greet(peer16(d))
-
+        for side in (core, 1 - core):
+            greet((g, slab_of(zh, plane_peer(d), side)))
+    for d in range(1, 8):
+        greet(at(z + d, plane, core))
     far_end = at(z + 4, 15 * (1 - core), 1 - core)
     greet(far_end)
 
@@ -128,7 +138,9 @@
 
         lax.fori_loop(0, 16, one, 0)
 
-    pl.semaphore_wait(barrier, 33 + jnp.where(edge, 16, 0))
+    for load in loads:
+        load.wait()
+    pl.semaphore_wait(barrier, 41 + jnp.where(edge, 16, 0))
 
     flow = [
         remote(v_ref, vleft, v_send.at[0], v_recv.at[0], (g, ahead)),
@@ -290,61 +302,79 @@
 
     lax.fori_loop(0, CHUNKS, gathered, 0)
 
-    def scatter(d):
+    def plane_device(p2, side):
+        return g, slab_of(zh, p2, side)
+
+    def swap():
+        return remote(part.at[pl.ds((1 - core) * 8, 8)], pair_buf, c_send, c_recv, partner)
+
+    def scatter(i):
+        p2 = core * 8 + i
+        return remote(part.at[p2], rs_buf.at[plane], p_send.at[i], p_recv.at[plane], plane_device(p2, core))
+
+    def spread(d):
+        return remote(tile, zbuf.at[z], z_send.at[d], z_recv.at[z], at(z + d, plane, core))
+
+    def share(d, side):
         p2 = plane_peer(d)
-        return remote(part.at[p2], rs_buf.at[plane], p_send.at[p2], p_recv.at[plane], (g, slab_of(zh, p2, core)))
-
-    def scatter_in(d):
-        p2 = plane_peer(d)
-        return remote(part.at[plane], rs_buf.at[p2], p_send.at[plane], p_recv.at[p2], (g, slab_of(zh, p2, core)))
-
-    slot = g * 4 + zh * 2 + core
-
-    def spread(d):
-        return remote(tile, zbuf.at[slot], z_send.at[d], z_recv.at[slot], peer16(d))
+        return remote(mine, coup_ref.at[plane], g_send.at[side, d], g_recv.at[plane], plane_device(p2, lax.rem(core + side, 2)))
+
+    def landed(ref, sem, i, skip):
+        @pl.when(jnp.logical_not(skip))
+        def _():
+            pltpu.make_async_copy(ref.at[i], ref.at[i], sem.at[i]).wait()
+
+    def hops(d):
+        return min(d // 4, 4 - d // 4) + min(d % 4, 4 - d % 4)
+
+    others = [(d, side) for side in range(2) for d in range(16) if d or side]
+    others.sort(key=lambda pair: -hops(pair[0]))
 
     def pair(k, q):
         return jnp.concatenate([quart[k, :, 2 * q + j].reshape(SNAP, 128) for j in range(2)], axis=1)
 
-    for k in range(3):
-
-        def product(q, total):
-            return total + lax.dot_general(
-                pair(3, q), pair(k, q), (((1,), (1,)), ((), ())), preferred_element_type=jnp.float32
-            )
-
-        total = lax.fori_loop(0, 4, product, jnp.zeros((SNAP, SNAP), jnp.float32))
+    def product(q, totals):
+        lhs = pair(3, q)
+        wide_two = jnp.concatenate([pair(0, q), pair(1, q)], axis=0)
+
+        def against(rhs):
+            return lax.dot_general(lhs, rhs, (((1,), (1,)), ((), ())), preferred_element_type=jnp.float32)
+
+        return totals[0] + against(wide_two), totals[1] + against(pair(2, q))
+
+    two, one_more = lax.fori_loop(
+        0, 4, product, (jnp.zeros((SNAP, 2 * SNAP), jnp.float32), jnp.zeros((SNAP, SNAP), jnp.float32))
+    )
+    for k, total in enumerate((two[:, :SNAP], two[:, SNAP:], one_more)):
         part[:, k] = total.reshape(16, 8, SNAP)
-    for d in range(1, 16):
-        scatter(d).start()
-    rs_buf[plane] = part[plane]
-    for d in range(1, 16):
-        scatter_in(d).wait_recv()
-    tile[...] = jnp.sum(rs_buf[...], axis=0)
-    for d in range(1, 16):
-        spread(d).start()
-    zbuf[slot] = tile[...]
-    for here in range(16):
-
-        @pl.when(slot != here)
-        def _():
-            pltpu.make_async_copy(zbuf.at[here], zbuf.at[here], z_recv.at[here]).wait()
-
-    mine[...] = jnp.sum(zbuf[...], axis=0) * scale
-
-    def share(d):
-        p2 = plane_peer(d)
-        return remote(mine, coup_ref.at[plane], g_send.at[p2], g_recv.at[plane], (g, slab_of(zh, p2, core)))
-
-    def share_in(d):
-        p2 = plane_peer(d)
-        return remote(mine, coup_ref.at[p2], g_send.at[plane], g_recv.at[p2], (g, slab_of(zh, p2, core)))
-
-    for d in range(1, 16):
-        share(d).start()
-    coup_ref[plane] = mine[...]
-    for d in range(1, 16):
-        share_in(d).wait_recv()
+    swap().start()
+    swap().wait_recv()
+    for i in range(8):
+        p2 = core * 8 + i
+        part[p2] += pair_buf[i]
+
+        @pl.when(p2 != plane)
+        def _():
+            scatter(i).start()
+
+    @pl.when(owner)
+    def _():
+        rs_buf[plane] = part[plane]
+        for i in range(16):
+            landed(rs_buf, p_recv, i, plane == i)
+        tile[...] = jnp.sum(rs_buf[...], axis=0)
+        for d in range(1, 8):
+            spread(d).start()
+        zbuf[z] = tile[...]
+        for i in range(8):
+            landed(zbuf, z_recv, i, z == i)
+        mine[...] = jnp.sum(zbuf[...], axis=0) * scale
+        for d, side in others:
+            share(d, side).start()
+        coup_ref[plane] = mine[...]
+
+    for i in range(16):
+        landed(coup_ref, g_recv, i, owner & (plane == i))
 
     root = invert(coup_ref, m_ref)
 
@@ -426,10 +456,20 @@
     def _():
         across(relay_buf, plane, y_send)[0].wait_send()
 
-    for d in range(1, 16):
-        scatter(d).wait_send()
-        spread(d).wait_send()
-        share(d).wait_send()
+    swap().wait_send()
+    for i in range(8):
+
+        @pl.when(core * 8 + i != plane)
+        def _():
+            scatter(i).wait_send()
+
+    @pl.when(owner)
+    def _():
+        for d in range(1, 8):
+            spread(d).wait_send()
+        for d, side in others:
+            share(d, side).wait_send()
+
     for kind in range(2):
         for d in range(1, 4):
             post(d, kind).wait_send()
@@ -494,9 +534,11 @@
     dm, am = pl.pallas_call(
         functools.partial(kernel, scale),
         out_shape=(modes, modes),
-        in_specs=[vmem] * 2,
+        in_specs=[pl.BlockSpec(memory_space=pltpu.HBM)] * 2,
         out_specs=(vmem,) * 2,
         scratch_shapes=[
+            pltpu.VMEM(slab_shape, bf16),
+            pltpu.VMEM(base_flow.shape, f32),
             pltpu.VMEM(slab_shape, bf16),
             pltpu.VMEM(slab_shape, bf16),
             pltpu.VMEM((8,) + slab_shape[1:], bf16),
@@ -508,14 +550,18 @@
             pltpu.VMEM((CHUNKS, 4, 8, PER, 128), bf16),
             pltpu.VMEM((4, CHUNKS, 8, PER, 128), bf16),
             pltpu.VMEM((16, 3, 8, SNAP), f32),
+            pltpu.VMEM((8, 3, 8, SNAP), f32),
             pltpu.VMEM((16, 3, 8, SNAP), f32),
             pltpu.VMEM((3, 8, SNAP), f32),
-            pltpu.VMEM((16, 3, 8, SNAP), f32),
+            pltpu.VMEM((8, 3, 8, SNAP), f32),
             pltpu.VMEM((3, 8, SNAP), f32),
             pltpu.VMEM((16, 3, 8, SNAP), f32),
             pltpu.VMEM((SNAP, SNAP), f32),
             pltpu.VMEM((3, SNAP, SNAP), bf16),
             pltpu.VMEM((2, 4, 8, 32, 128), bf16),
+            dma((2,)),
+            dma,
+            dma,
             dma((2, CHUNKS)),
             dma((2, CHUNKS)),
             dma((2,)),
@@ -526,17 +572,17 @@
             dma,
             dma((CHUNKS, 4)),
             dma((4, CHUNKS)),
+            dma((8,)),
             dma((16,)),
-            dma((16,)),
-            dma((16,)),
-            dma((16,)),
-            dma((16,)),
+            dma((8,)),
+            dma((8,)),
+            dma((2, 16)),
             dma((16,)),
             dma((2, 4)),
             dma((2, 4)),
         ],
         compiler_params=pltpu.CompilerParams(
-            collective_id=0, has_side_effects=True, vmem_limit_bytes=48 * MIB
+            collective_id=0, has_side_effects=True, vmem_limit_bytes=59 * MIB
         ),
         name="pod",
     )(field, base_flow)

time: 84.8 us -> 82.8 us (0.976)
  Pallas kernels: 80.4 us -> 79.1 us
  local copies, waits for them, and re-layouts: 2.93 us -> 2.02 us
    unnamed x4 -> x0, local copies, waits for them, and re-layouts: 1.93 us -> none
    pallas_call x1, Pallas kernels: 80.4 us -> 79.1 us  [per_device(): pl.pallas_call(functools.partial(kernel, scale), out_shape=(modes, modes)...]
    transpose x1, local copies, waits for them, and re-layouts: 0.99 us -> 2.02 us  [placed(): return x.reshape(4, 8, 32, 128).transpose(2, 0, 1, 3)]
where the time goes in v4:
time: 82.8 us; the launch traced here: 81.7 us
  Pallas kernels  79.1 us (96%)
  local copies, waits for them, and re-layouts  2.02 us (2%)
    pallas_call x1, Pallas kernels, per_device(): pl.pallas_call(functools.partial(kernel, scale), out_shape=(modes, modes)...  79.1 us
    transpose x1, local copies, waits for them, and re-layouts, placed(): return x.reshape(4, 8, 32, 128).transpose(2, 0, 1, 3)  2.02 us

profile of v4, /device:TPU:64, one launch (start us, length us, event | category | flops | bytes accessed | tf_op | source)
XLA Modules:
  0.0 81.7 jit_solution(12450102695069470712)
XLA Ops:
  0.6 79.1 %pod.1 = (bf16[32,32,128]{2,1,0:T(8,128)(2,1)}, bf16[32,32,128]{2,1,0:T(8,128)(2,1)}) custom-call(bf16[128,4,8,128]{3,2,1,0:T(8,128)(2,1)} %bitcast.7, f32[4,8,128]{2,1,0:T(8,128)} %v_hbm.1), custom_call_target="tpu_custom_call" | custom-call | tf_op jit(solution)/shard_map/pod/pallas_call | solution.py:534
  79.7 2.0 %copy_bitcast_fusion = (bf16[32,4,8,128]{3,2,1,0:T(8,128)(2,1)}, bf16[32,4,8,128]{3,2,1,0:T(8,128)(2,1)}) fusion(bf16[4,8,32,128]{3,2,1,0:T(8,128)(2,1)} %bitcast.9, bf16[4,8,32,128]{3,2,1,0:T(8,128)(2,1)} %bitcast.8), kind=kLoop, calls=%fused_computation | loop fusion | bytes 1048576 | tf_op jit(solution)/shard_map/transpose | solution.py:591

commit v5 on v4

--- a/solution.py
+++ b/solution.py
@@ -288,7 +288,8 @@
 
         for q in range(32):
             own[c, q // 8, q % 8] = packed(q)
-        for d in range(1, 4):
+        odd = lax.rem(g, 2)
+        for d in (2, 3 - 2 * odd, 1 + 2 * odd):
             piece(c, d).start()
         quart[g, c] = own[c, g]
         return carry

time: 82.8 us -> 82.9 us (level)
  no operation moved by 1% of the time
where the time goes in v5:
time: 82.9 us; the launch traced here: 81.4 us
  Pallas kernels  78.7 us (95%)
  local copies, waits for them, and re-layouts  2.02 us (2%)
    pallas_call x1, Pallas kernels, per_device(): pl.pallas_call(functools.partial(kernel, scale), out_shape=(modes, modes)...  78.7 us
    transpose x1, local copies, waits for them, and re-layouts, placed(): return x.reshape(4, 8, 32, 128).transpose(2, 0, 1, 3)  2.02 us

profile of v5, /device:TPU:64, one launch (start us, length us, event | category | flops | bytes accessed | tf_op | source)
XLA Modules:
  0.0 81.4 jit_solution(1538376947969590861)
XLA Ops:
  0.6 78.7 %pod.1 = (bf16[32,32,128]{2,1,0:T(8,128)(2,1)}, bf16[32,32,128]{2,1,0:T(8,128)(2,1)}) custom-call(bf16[128,4,8,128]{3,2,1,0:T(8,128)(2,1)} %bitcast.7, f32[4,8,128]{2,1,0:T(8,128)} %v_hbm.1), custom_call_target="tpu_custom_call" | custom-call | tf_op jit(solution)/shard_map/pod/pallas_call | solution.py:535
  79.3 2.0 %copy_bitcast_fusion = (bf16[32,4,8,128]{3,2,1,0:T(8,128)(2,1)}, bf16[32,4,8,128]{3,2,1,0:T(8,128)(2,1)}) fusion(bf16[4,8,32,128]{3,2,1,0:T(8,128)(2,1)} %bitcast.9, bf16[4,8,32,128]{3,2,1,0:T(8,128)(2,1)} %bitcast.8), kind=kLoop, calls=%fused_computation | loop fusion | bytes 1048576 | tf_op jit(solution)/shard_map/transpose | solution.py:592
